TPU v7x, 256 devices: a 8x8x2 block of a 8x8x16 slice. The times are simulated.
256 devices in a mesh: groups: 2 (over z), tp: 16 (over x, core), dp: 8 (over y).
Axes of the slice: x: 8, y: 8, z: 2, core: 2. Of those that a mesh axis runs over, the one named last changes fastest.
The devices are a block of a 8x8x16 slice.
Arguments:
- hidden: bfloat16 [256, 2560], P(('groups', 'dp'), 'tp'), parts along dimension 0, may hold values from -40 to 40
- in_gain: float32 [2560], replicated, may hold values from 0.1 to 1.9
- z_weight: bfloat16 [2560, 5120], P(None, 'tp'), may hold values from -0.125 to 0.125
- x_weight: bfloat16 [2560, 5120], P(None, 'tp'), may hold values from -0.125 to 0.125
- bc_weight: bfloat16 [2560, 256], P(None, 'tp'), may hold values from -0.125 to 0.125
- dt_weight: bfloat16 [2560, 80], P(None, 'tp'), may hold values from -0.125 to 0.125
- conv_x_weight: bfloat16 [4, 5120], P(None, 'tp'), may hold values from -3 to 3
- conv_x_bias: bfloat16 [5120], P('tp'), may hold values from -3 to 3
- conv_bc_weight: bfloat16 [4, 256], P(None, 'tp'), may hold values from -3 to 3
- conv_bc_bias: bfloat16 [256], P('tp'), may hold values from -3 to 3
- conv_x_state: bfloat16 [256, 3, 5120], P(('groups', 'dp'), None, 'tp'), parts along dimension 0, may hold values from -6 to 6
- conv_bc_state: bfloat16 [256, 3, 256], P(('groups', 'dp'), None, 'tp'), parts along dimension 0, may hold values from -6 to 6
- dt_bias: float32 [80], P('tp'), may hold values from -4 to -1
- log_rate: float32 [80], P('tp'), may hold values from 0 to 2.5
- skip_gain: float32 [80], P('tp'), may hold values from 0.5 to 2
- ssm_state: float32 [256, 80, 64, 128], P(('groups', 'dp'), 'tp'), parts along dimension 0, may hold values from -20 to 20
- norm_gain: float32 [5120], P('tp'), may hold values from 0.1 to 1.9
- out_weight: bfloat16 [5120, 2560], P('tp'), may hold values from -0.125 to 0.125
- pool_slot: int32 [16, 16], P(('groups', 'dp')), parts along dimension 0, may hold values from 0 to 15, as said below
- active: int32 [256], P(('groups', 'dp')), parts along dimension 0, may hold values 0 or 1
Outputs:
- layer_out: bfloat16 [256, 2560], P(('groups', 'dp'), 'tp'), parts along dimension 0
- conv_x_next: bfloat16 [256, 3, 5120], P(('groups', 'dp'), None, 'tp'), parts along dimension 0
- conv_bc_next: bfloat16 [256, 3, 256], P(('groups', 'dp'), None, 'tp'), parts along dimension 0
- ssm_next: float32 [256, 80, 64, 128], P(('groups', 'dp'), 'tp'), parts along dimension 0
There are 2 independent parts, one for each index of `groups`. A program takes and returns all parts, laid end to end along the dimension named above; an argument that names none is the same for every part. Nothing has to cross between parts.
Inputs may be any that keep to these rules, and one draw needn't show every extreme that they name: `pool_slot`: each row is a permutation of 0 to 15.
All inputs are finite; a program needn't handle non-finite values. No bound on the sum of `active` on one device may be relied on, other than what follows from the above.
Results may differ from a plain program's by a relative error of at most 0.0085.
Values may be sent and summed in bfloat16 or wider, within the bound.
A program may use at most 64 MiB of HBM per device.

v0:
```python
import jax
import jax.numpy as jnp
from jax import lax
from jax.sharding import PartitionSpec as P

HP = 64
NS = 128
INNER = 5120


def in_order(tiles, dim):
    dims = list(tiles.shape[1:])
    dims[dim] *= tiles.shape[0]
    return jnp.moveaxis(tiles, 0, dim).reshape(dims)


def from_everyone(x, axis):
    length = lax.axis_size(axis)
    return lax.all_to_all(jnp.broadcast_to(x[None], (length, *x.shape)), axis, 0, 0, tiled=True)


def gathered_copies(x, axis, dim):
    return in_order(from_everyone(x, axis), dim)


def over_copies(x, axis):
    return from_everyone(x, axis).sum(axis=0)


def in_blocks(x, dim, length):
    dims = x.shape
    tiles = x.reshape(*dims[:dim], length, dims[dim] // length, *dims[dim + 1 :])
    return jnp.moveaxis(tiles, dim, 0)


def summed_on_arrival(x, axis, dim):
    tiles = in_blocks(x, dim, lax.axis_size(axis))
    arrived = lax.all_to_all(tiles, axis, split_axis=0, concat_axis=0, tiled=True)
    return arrived.sum(axis=0)


def convolve(old_state, current, weight, conv_bias):
    window = jnp.concatenate(
        [old_state.astype(jnp.float32), current.astype(jnp.float32)[:, None, :]], axis=1
    )
    conv_out = jnp.sum(window * weight.astype(jnp.float32)[None], axis=1) + conv_bias.astype(
        jnp.float32
    )
    return (jax.nn.silu(conv_out).astype(jnp.bfloat16), window[:, 1:, :].astype(jnp.bfloat16))


def shards(
    hidden,
    in_gain,
    z_weight,
    x_weight,
    bc_weight,
    dt_weight,
    conv_x_weight,
    conv_x_bias,
    conv_bc_weight,
    conv_bc_bias,
    conv_x_state,
    conv_bc_state,
    dt_bias,
    log_rate,
    skip_gain,
    ssm_state,
    norm_gain,
    out_weight,
    pool_slot,
    active,
):
    seq_rows = hidden.shape[0]
    hidden_f32 = hidden.astype(jnp.float32)
    owner_slot = pool_slot.reshape(-1)
    requests = jnp.arange(seq_rows, dtype=jnp.int32)
    onehot = owner_slot[:, None] == requests[None, :]
    at_slot = jnp.sum(jnp.where(onehot, requests[:, None], 0), axis=0)
    bc_matrix, bc_taps, bc_shift, bc_old = (bc_weight, conv_bc_weight, conv_bc_bias, conv_bc_state)
    matrices = (z_weight, x_weight, bc_matrix, dt_weight)
    whole_rows = gathered_copies(hidden, "tp", 1).astype(jnp.float32)
    inv_rms = lax.rsqrt(jnp.mean(whole_rows * whole_rows, axis=1, keepdims=True) + 1e-05)
    normed = (whole_rows * inv_rms * in_gain).astype(jnp.bfloat16)
    proj_sums = tuple(
        (jnp.dot(normed, matrix, preferred_element_type=jnp.float32) for matrix in matrices)
    )
    z_proj, x_proj, bc_proj, dt_proj = (part_sum.astype(jnp.bfloat16) for part_sum in proj_sums)
    is_live = active[at_slot] > 0
    x_conv, x_kept = convolve(conv_x_state, x_proj[at_slot], conv_x_weight, conv_x_bias)
    conv_x_next = jnp.where(is_live[:, None, None], x_kept, conv_x_state)
    bc_conv, bc_kept = convolve(bc_old, bc_proj[at_slot], bc_taps, bc_shift)
    bc_full = gathered_copies(bc_conv, "tp", 1)
    conv_bc_next = jnp.where(is_live[:, None, None], bc_kept, conv_bc_state)
    b_rows = bc_full[:, :NS].astype(jnp.float32)
    c_rows = bc_full[:, NS:].astype(jnp.float32)
    dt_step = jax.nn.softplus(dt_proj[at_slot].astype(jnp.float32) + dt_bias)
    decay_rate = jnp.exp(-dt_step * jnp.exp(log_rate))
    heads_dev = ssm_state.shape[1]
    x_heads = x_conv.astype(jnp.float32).reshape(seq_rows, heads_dev, HP)
    fresh_state = (
        decay_rate[:, :, None, None] * ssm_state
        + (dt_step[:, :, None] * x_heads)[:, :, :, None] * b_rows[:, None, None, :]
    )
    fresh_state = jnp.where(is_live[:, None, None, None], fresh_state, ssm_state)
    y_slot = jnp.einsum("bhpn,bn->bhp", fresh_state, c_rows) + skip_gain[None, :, None] * x_heads
    y_request = y_slot.reshape(seq_rows, heads_dev * HP)[owner_slot]
    gated_y = y_request * jax.nn.silu(z_proj.astype(jnp.float32))
    part_sq = jnp.sum(gated_y * gated_y, axis=1)
    scaled = (gated_y * norm_gain).astype(jnp.bfloat16)
    branch_part = jnp.dot(scaled, out_weight, preferred_element_type=jnp.float32)
    sq_total = over_copies(part_sq, "tp")
    branch_sum = summed_on_arrival(branch_part, "tp", 1)
    inv_out = lax.rsqrt(sq_total / INNER + 1e-05)
    live_request = active > 0
    layer_out = jnp.where(
        live_request[:, None],
        (hidden_f32 + inv_out[:, None] * branch_sum).astype(jnp.bfloat16),
        hidden,
    )
    return (layer_out, conv_x_next, conv_bc_next, fresh_state)


def solution(mesh):
    placed = (
        P(("groups", "dp"), "tp"),
        P(),
        P(None, "tp"),
        P(None, "tp"),
        P(None, "tp"),
        P(None, "tp"),
        P(None, "tp"),
        P("tp"),
        P(None, "tp"),
        P("tp"),
        P(("groups", "dp"), None, "tp"),
        P(("groups", "dp"), None, "tp"),
        P("tp"),
        P("tp"),
        P("tp"),
        P(("groups", "dp"), "tp", None, None),
        P("tp"),
        P("tp", None),
        P(("groups", "dp"), None),
        P(("groups", "dp")),
    )
    return jax.shard_map(
        shards,
        mesh=mesh,
        in_specs=placed,
        out_specs=(
            P(("groups", "dp"), "tp"),
            P(("groups", "dp"), None, "tp"),
            P(("groups", "dp"), None, "tp"),
            P(("groups", "dp"), "tp", None, None),
        ),
        check_vma=False,
    )
```

profile of v0, /device:TPU:513, one launch (start us, length us, event | category | flops | bytes accessed | tf_op | source)
XLA Modules:
  0.0 94.7 jit_solution(9188188251485929307)
XLA Ops:
  0.7 1.5 %broadcast_in_dim.48 = bf16[16,16,160]{2,1,0:T(8,128)(2,1)} broadcast(bf16[16,160]{1,0:T(8,128)(2,1)} %param.20), dimensions={1,2} | broadcast | bytes 87040 | tf_op jit(solution)/shard_map/broadcast_in_dim | solution.py:19
  2.2 23.7 %all-to-all-start = ((bf16[16,16,160]{2,1,0:T(8,128)(2,1)}), bf16[16,16,160]{2,1,0:T(8,128)(2,1)S(1)}, u32[]{:S(2)}, u32[]{:S(2)}) async-start(bf16[16,16,160]{2,1,0:T(8,128)(2,1)} %broadcast_in_dim.48), calls=%async_computation | async-start | bytes 262144 | tf_op jit(solution)/shard_map/all_to_all | solution.py:19
  25.9 0.7 fusion.13
  26.6 0.7 select_reduce_fusion
  27.3 1.2 %broadcast_compare_fusion.1 = pred[16]{0:T(512)(128)(4,1)} fusion(s32[16]{0:T(128)} %param.39), kind=kLoop, calls=%fused_computation.57 | loop fusion | flops 16 | bytes 80 | tf_op jit(solution)/shard_map/gt | solution.py:115
  28.5 1.3 %gather_fusion = s32[16]{0:T(128)S(1)} fusion(s32[16]{0:T(128)} %param.39, s32[1024]{0:T(1024)S(1)} %pad_clamp_fusion.1), kind=kCustom, calls=%fused_computation | custom fusion | bytes 192 | tf_op jit(solution)/shard_map/gather | solution.py:89
  30.4 0.7 convert_element_type.124
  31.1 1.2 %exp.43 = f32[5]{0:T(128)} exponential(f32[5]{0:T(128)} %param.33) | non-fusion elementwise | bytes 40 | tf_op jit(solution)/shard_map/exp | solution.py:98
  32.3 0.8 reshape.228
  33.1 1.3 %convert_element_type.129 = f32[4,16]{1,0:T(4,128)} convert(bf16[4,16]{1,0:T(4,128)(2,1)} %param.28) | non-fusion elementwise | flops 64 | bytes 384 | tf_op jit(solution)/shard_map/convert_element_type | solution.py:46
  34.3 1.2 %convert_element_type.130 = f32[16]{0:T(128)} convert(bf16[16]{0:T(256)(128)(2,1)} %param.29) | non-fusion elementwise | flops 16 | bytes 96 | tf_op jit(solution)/shard_map/convert_element_type | solution.py:46
  36.1 0.9 copy.37
  37.0 1.8 %reshape.227 = f32[16,2560]{1,0:T(8,128)} reshape(f32[16,16,160]{2,1,0:T(8,128)} %copy.37) | data formatting | bytes 327680 | tf_op jit(solution)/shard_map/convert_element_type | solution.py:82
  39.0 1.0 %multiply_convert_fusion = bf16[16,2560]{1,0:T(8,128)(2,1)S(1)} fusion(f32[16,2560]{1,0:T(8,128)} %reshape.227, f32[2560]{0:T(1024)} %param.21, f32[16]{0:T(128)S(1)} %add_rsqrt_fusion.1), kind=kLoop, calls=%fused_computation.15 | loop fusion | flops 122880 | bytes 256064 | tf_op jit(solution)/shard_map/convert_element_type | solution.py:84
  41.2 0.9 convolution_convert_fusion.3
  42.8 1.0 %convolution_convert_fusion.2 = bf16[16,16]{1,0:T(8,128)(2,1)S(1)} fusion(bf16[16,2560]{1,0:T(8,128)(2,1)S(1)} %multiply_convert_fusion, bf16[2560,16]{0,1:T(8,128)(2,1)} %param.24), kind=kOutput, calls=%fused_computation.9 | convolution fusion | flops 1310976 | bytes 164352 | tf_op jit(solution)/shard_map/dot_general | solution.py:86
  44.5 0.7 reshape.271
  45.2 7.4 %all-to-all-start.1 = ((bf16[16,2,128]{2,1,0:T(2,128)(2,1)}), bf16[16,2,128]{2,1,0:T(2,128)(2,1)S(1)}, u32[]{:S(2)}, u32[]{:S(2)}) async-start(bf16[16,2,128]{2,1,0:T(2,128)(2,1)} %reshape.271), calls=%async_computation.1 | async-start | bytes 16384 | tf_op jit(solution)/shard_map/all_to_all | solution.py:19
  52.7 0.7 fusion.4
  53.4 6.1 %all-to-all-done.1 = bf16[16,2,128]{2,1,0:T(2,128)(2,1)S(1)} async-done(((bf16[16,2,128]{2,1,0:T(2,128)(2,1)}), bf16[16,2,128]{2,1,0:T(2,128)(2,1)S(1)}, u32[]{:S(2)}, u32[]{:S(2)}) %all-to-all-start.1) | async-done | bytes 8224 | tf_op jit(solution)/shard_map/all_to_all | solution.py:19
  59.8 2.3 %add_select_fusion = f32[16,5,64,128]{3,2,1,0:T(8,128)S(1)} fusion(f32[16,5,64,128]{3,2,1,0:T(8,128)} %param.35, f32[16,128]{1,0:T(8,128)S(1)} %get-tuple-element.5, f32[16,5,64]{2,1,0:T(8,128)S(1)} %convert_multiply_fusion.2, f32[16,5]{1,0:T(8,128)S(1)} %get-tuple-element.6, pred[16]{0:T(512)(128)(4,1)S(1)} %copy-done.8), kind=kLoop, calls=%fused_computation.5 | loop fusion | flops 2621440 | bytes 5271888 | tf_op jit(solution)/shard_map/jit(_where)/select_n | solution.py:105
  62.2 1.4 %copy-done.1 = f32[16,5,64,128]{3,2,1,0:T(8,128)} copy-done((f32[16,5,64,128]{3,2,1,0:T(8,128)}, f32[16,5,64,128]{3,2,1,0:T(8,128)S(1)}, u32[]{:S(2)}) %copy-start.1) | copy-done | bytes 2621464
  63.6 1.0 %fusion.10 = f32[16,1,5,64]{3,1,2,0:T(1,128)S(1)} fusion(f32[16,5,64,128]{3,2,1,0:T(8,128)S(1)} %add_select_fusion, bf16[16,128,1,1]{1,0,2,3:T(8,128)(2,1)S(1)} %get-tuple-element.4), kind=kOutput, calls=%fused_computation.40 | convolution fusion | flops 1310720 | bytes 2646016 | tf_op jit(solution)/shard_map/bhpn,bn->bhp/dot_general | solution.py:106
  64.8 0.8 gather_fusion.4
  65.7 0.7 multiply_reduce_fusion.2
  67.0 3.9 %all-to-all-start.2 = ((f32[16,1,16]{2,1,0:T(1,128)}), f32[16,1,16]{2,1,0:T(1,128)S(1)}, u32[]{:S(2)}, u32[]{:S(2)}) async-start(f32[16,1,16]{2,1,0:T(1,128)} %broadcast_in_dim.50), calls=%async_computation.2 | async-start | bytes 16384 | tf_op jit(solution)/shard_map/all_to_all | solution.py:19
  71.4 0.9 copy.48
  72.3 5.7 %all-to-all-done.2 = f32[16,1,16]{2,1,0:T(1,128)S(1)} async-done(((f32[16,1,16]{2,1,0:T(1,128)}), f32[16,1,16]{2,1,0:T(1,128)S(1)}, u32[]{:S(2)}, u32[]{:S(2)}) %all-to-all-start.2) | async-done | bytes 1056 | tf_op jit(solution)/shard_map/all_to_all | solution.py:19
  78.0 4.0 %all-to-all-start.3 = ((f32[16,16,160]{2,1,0:T(8,128)}), f32[16,16,160]{2,1,0:T(8,128)S(1)}, u32[]{:S(2)}, u32[]{:S(2)}) async-start(f32[16,16,160]{2,1,0:T(8,128)} %bitcast.31), calls=%async_computation.3 | async-start | bytes 524288 | tf_op jit(solution)/shard_map/all_to_all | solution.py:38
  82.0 0.7 fusion.7
  82.7 11.3 %all-to-all-done.3 = f32[16,16,160]{2,1,0:T(8,128)S(1)} async-done(((f32[16,16,160]{2,1,0:T(8,128)}), f32[16,16,160]{2,1,0:T(8,128)S(1)}, u32[]{:S(2)}, u32[]{:S(2)}) %all-to-all-start.3) | async-done | bytes 163872 | tf_op jit(solution)/shard_map/all_to_all | solution.py:38
  94.0 0.7 fusion.5
  (63 shorter events, 5.7 us)
Async XLA Ops:
  0.6 70.3 %copy-start = (bf16[320,2560]{1,0:T(8,128)(2,1)S(1)}, bf16[320,2560]{1,0:T(8,128)(2,1)}, u32[]{:S(2)}) copy-start(bf16[320,2560]{1,0:T(8,128)(2,1)} %param.37) | copy-start | bytes 4915204
  0.6 39.3 %copy-start.2 = (bf16[2560,320]{0,1:T(8,128)(2,1)S(1)}, bf16[2560,320]{0,1:T(8,128)(2,1)}, u32[]{:S(2)}) copy-start(bf16[2560,320]{0,1:T(8,128)(2,1)} %param.23) | copy-start | bytes 4915204
  0.7 40.5 %copy-start.4 = (bf16[16,3,320]{2,0,1:T(8,128)(2,1)S(1)}, bf16[16,3,320]{2,0,1:T(8,128)(2,1)}, u32[]{:S(2)}) copy-start(bf16[16,3,320]{2,0,1:T(8,128)(2,1)} %param.30) | copy-start | bytes 92164
  0.7 43.8 %copy-start.5 = (bf16[16,3,16]{2,0,1:T(8,128)(2,1)S(1)}, bf16[16,3,16]{2,0,1:T(8,128)(2,1)}, u32[]{:S(2)}) copy-start(bf16[16,3,16]{2,0,1:T(8,128)(2,1)} %param.31) | copy-start | bytes 4612
  2.2 33.9 %all-to-all-start = ((bf16[16,16,160]{2,1,0:T(8,128)(2,1)}), bf16[16,16,160]{2,1,0:T(8,128)(2,1)S(1)}, u32[]{:S(2)}, u32[]{:S(2)}) async-start(bf16[16,16,160]{2,1,0:T(8,128)(2,1)} %broadcast_in_dim.48), calls=%async_computation | async-start | bytes 262144 | tf_op jit(solution)/shard_map/all_to_all | solution.py:19
  38.9 5.5 %copy-start.7 = (f32[4,16]{1,0:T(4,128)S(1)}, f32[4,16]{1,0:T(4,128)}, u32[]{:S(2)}) copy-start(f32[4,16]{1,0:T(4,128)} %convert_element_type.129) | copy-start | bytes 772
  38.9 5.6 %copy-start.15 = (f32[16]{0:T(128)S(1)}, f32[16]{0:T(128)}, u32[]{:S(2)}) copy-start(f32[16]{0:T(128)} %convert_element_type.130) | copy-start | bytes 196
  38.9 13.7 %copy-start.13 = (f32[5]{0:T(128)S(1)}, f32[5]{0:T(128)}, u32[]{:S(2)}) copy-start(f32[5]{0:T(128)} %param.32) | copy-start | bytes 64
  38.9 13.7 %copy-start.14 = (f32[5]{0:T(128)S(1)}, f32[5]{0:T(128)}, u32[]{:S(2)}) copy-start(f32[5]{0:T(128)} %exp.43) | copy-start | bytes 64
  38.9 13.8 %copy-start.8 = (pred[16]{0:T(512)(128)(4,1)S(1)}, pred[16]{0:T(512)(128)(4,1)}, u32[]{:S(2)}) copy-start(pred[16]{0:T(512)(128)(4,1)} %broadcast_compare_fusion) | copy-start | bytes 52
  45.2 14.3 %all-to-all-start.1 = ((bf16[16,2,128]{2,1,0:T(2,128)(2,1)}), bf16[16,2,128]{2,1,0:T(2,128)(2,1)S(1)}, u32[]{:S(2)}, u32[]{:S(2)}) async-start(bf16[16,2,128]{2,1,0:T(2,128)(2,1)} %reshape.271), calls=%async_computation.1 | async-start | bytes 16384 | tf_op jit(solution)/shard_map/all_to_all | solution.py:19
  62.1 1.5 %copy-start.1 = (f32[16,5,64,128]{3,2,1,0:T(8,128)}, f32[16,5,64,128]{3,2,1,0:T(8,128)S(1)}, u32[]{:S(2)}) copy-start(f32[16,5,64,128]{3,2,1,0:T(8,128)S(1)} %add_select_fusion) | copy-start | bytes 7864324
  62.1 2.5 %copy-start.11 = (f32[5]{0:T(128)S(1)}, f32[5]{0:T(128)}, u32[]{:S(2)}) copy-start(f32[5]{0:T(128)} %param.34) | copy-start | bytes 64
  62.2 3.5 %copy-start.3 = (bf16[2560,320]{0,1:T(8,128)(2,1)S(1)}, bf16[2560,320]{0,1:T(8,128)(2,1)}, u32[]{:S(2)}) copy-start(bf16[2560,320]{0,1:T(8,128)(2,1)} %param.22) | copy-start | bytes 4915204
  62.2 8.8 %copy-start.10 = (f32[320]{0:T(512)S(1)}, f32[320]{0:T(512)}, u32[]{:S(2)}) copy-start(f32[320]{0:T(512)} %param.36) | copy-start | bytes 3844
  64.8 17.2 %copy-start.9 = (pred[16]{0:T(512)(128)(4,1)S(1)}, pred[16]{0:T(512)(128)(4,1)}, u32[]{:S(2)}) copy-start(pred[16]{0:T(512)(128)(4,1)} %broadcast_compare_fusion) | copy-start | bytes 52
  65.7 28.3 %copy-start.6 = (bf16[16,160]{1,0:T(8,128)(2,1)S(1)}, bf16[16,160]{1,0:T(8,128)(2,1)}, u32[]{:S(2)}) copy-start(bf16[16,160]{1,0:T(8,128)(2,1)} %param.20) | copy-start | bytes 15364
  65.7 28.3 %copy-start.12 = (pred[16]{0:T(512)(128)(4,1)S(1)}, pred[16]{0:T(512)(128)(4,1)}, u32[]{:S(2)}) copy-start(pred[16]{0:T(512)(128)(4,1)} %broadcast_compare_fusion.1) | copy-start | bytes 52
  67.0 11.0 %all-to-all-start.2 = ((f32[16,1,16]{2,1,0:T(1,128)}), f32[16,1,16]{2,1,0:T(1,128)S(1)}, u32[]{:S(2)}, u32[]{:S(2)}) async-start(f32[16,1,16]{2,1,0:T(1,128)} %broadcast_in_dim.50), calls=%async_computation.2 | async-start | bytes 16384 | tf_op jit(solution)/shard_map/all_to_all | solution.py:19
  78.0 16.0 %all-to-all-start.3 = ((f32[16,16,160]{2,1,0:T(8,128)}), f32[16,16,160]{2,1,0:T(8,128)S(1)}, u32[]{:S(2)}, u32[]{:S(2)}) async-start(f32[16,16,160]{2,1,0:T(8,128)} %bitcast.31), calls=%async_computation.3 | async-start | bytes 524288 | tf_op jit(solution)/shard_map/all_to_all | solution.py:38
where the time goes:
time: 95.4 us; the launch traced here: 94.7 us
  starting transfers between devices  39 us (41%)
  waiting for transfers between devices  23.1 us (24%)
  local copies, waits for them, and re-layouts  14.4 us (15%)
  other arithmetic  12.7 us (13%)
  matrix products  4.49 us (5%)
  between operations  0.96 us (1%)
    all_to_all x3, starting transfers between devices, from_everyone(): lax.all_to_all(jnp.broadcast_to(x[None], (length, *x.shape)), axis, 0, 0,...  35 us
    all_to_all x3, waiting for transfers between devices, from_everyone(): lax.all_to_all(jnp.broadcast_to(x[None], (length, *x.shape)), axis, 0, 0,...  11.8 us
    all_to_all x1, waiting for transfers between devices, summed_on_arrival(): lax.all_to_all(tiles, axis, split_axis=0, concat_axis=0, tiled=True)  11.3 us
    all_to_all x1, starting transfers between devices, summed_on_arrival(): lax.all_to_all(tiles, axis, split_axis=0, concat_axis=0, tiled=True)  4 us
    dot_general x4, matrix products, shards(): jnp.dot(normed, matrix, preferred_element_type=jnp.float32)  3.1 us
    convert_element_type x2, local copies, waits for them, and re-layouts, shards(): whole_rows = gathered_copies(hidden, 'tp', 1).astype(jnp.float32)  2.63 us
    unnamed x34, local copies, waits for them, and re-layouts  2.33 us
    select_n x1, other arithmetic, shards(): jnp.where(is_live[:, None, None, None], fresh_state, ssm_state)  2.31 us
  transfers between devices with their start and end apart: 4, of which 3 were waited for; matrix products, arithmetic and copies ran while one was open for 14% of the time, Pallas kernels for 0%

commit v1 on v0

v1 whole, which is shorter than its diff:
```python
import jax
import jax.numpy as jnp
from jax import lax
from jax.experimental import pallas as pl
from jax.experimental.pallas import tpu as pltpu
from jax.sharding import PartitionSpec as P

HP = 64
NS = 128
INNER = 5120
EPS = 1e-05
F32 = jnp.float32
BF16 = jnp.bfloat16
LANES = 128

NT = (((1,), (1,)), ((), ()))


def dot(a, b):
    return jnp.dot(a, b, preferred_element_type=F32)


def dot_nt(a, b):
    return lax.dot_general(a, b, NT, preferred_element_type=F32)


def iota(shape, dim):
    return lax.broadcasted_iota(jnp.int32, shape, dim)


def eye(n):
    return (iota((n, n), 0) == iota((n, n), 1)).astype(F32).astype(BF16)


def silu(x):
    return x * jax.nn.sigmoid(x)


def make_kernel(n_tp, seqs, feats, heads, chans, bc_dev):
    width = n_tp * feats
    tiles = width // LANES
    chips = n_tp // 2
    half = chips // 2
    offsets = []
    for far in range(half, 0, -1):
        for sign in (1, -1) if far < half or chips % 2 else (1,):
            for flip in (1, 0):
                offsets.append((sign * far, flip))
    offsets.append((0, 1))

    def body(
        hid, slot, act, in_gain, z_w, x_w, bc_w, dt_w, cx_w, cx_b, cbc_w, cbc_b, cx_s, cbc_s,
        dt_bias, log_rate, skip_gain, state, norm_gain, out_w,
        out_layer, out_cx, out_cbc, out_state,
        zw, xw, bcw, dtw, cxs, cbcs, st, ow, gain, stb, xn,
        hid_send, hid_recv, bc_send, bc_recv, sq_send, sq_recv, br_send, br_recv,
        in_sem, out_sem, send_sem, recv_sem,
    ):
        me = lax.axis_index("tp")
        chip, core = me // 2, lax.rem(me, 2)

        def partner(step, flip):
            return lax.rem(chip + step + chips, chips) * 2 + lax.rem(core + flip, 2)

        def local(i, src, dst):
            return pltpu.make_async_copy(src, dst, in_sem.at[i])

        barrier = pltpu.get_barrier_semaphore()
        for step, flip in offsets:
            pl.semaphore_signal(
                barrier, inc=1, device_id={"tp": partner(step, flip)}, device_id_type=pl.DeviceIdType.MESH
            )
        loads = [
            local(0, bc_w, bcw),
            local(1, dt_w, dtw),
            local(2, in_gain, gain),
            local(3, cbc_s, cbcs),
            local(4, z_w, zw),
            local(5, x_w, xw),
            local(6, cx_s, cxs),
            local(7, state, st),
            local(8, out_w, ow),
        ]
        for copy in loads:
            copy.start()

        def exchange(phase, src_of, dst_of, to):
            sends = []
            for j, (step, flip) in enumerate(offsets):
                peer = partner(step, flip)
                sends.append(
                    pltpu.make_async_remote_copy(
                        src_ref=src_of(peer), dst_ref=dst_of(me),
                        send_sem=send_sem.at[phase, j], recv_sem=recv_sem.at[phase, j],
                        device_id={"tp": peer}, device_id_type=pl.DeviceIdType.MESH,
                    )
                )
            for copy in sends:
                copy.start()
            return sends

        def arrive(phase, src_of, dst_of):
            for j, (step, flip) in enumerate(offsets):
                source = partner(-step, flip)
                pltpu.make_async_remote_copy(
                    src_ref=src_of(source), dst_ref=dst_of(source),
                    send_sem=send_sem.at[phase, j], recv_sem=recv_sem.at[phase, j],
                    device_id={"tp": source}, device_id_type=pl.DeviceIdType.MESH,
                ).wait_recv()

        slot_row = slot[...]
        act_row = act[...]
        by_slot = iota((seqs, seqs), 0) == jnp.broadcast_to(slot_row, (seqs, seqs))
        to_slot = by_slot.astype(F32).astype(BF16)
        shift = lax.rem(me * feats, LANES)
        place = (iota((feats, 2 * LANES), 1) == iota((feats, 2 * LANES), 0) + shift).astype(F32).astype(BF16)
        mine = dot(to_slot, hid[...]).astype(BF16)
        window = dot(mine, place).astype(BF16)
        hid_send[0] = window[:, :LANES]
        hid_send[1] = window[:, LANES:]
        pl.semaphore_wait(barrier, len(offsets))
        hid_out = exchange(0, lambda peer: hid_send, lambda who: hid_recv.at[who], 0)
        hid_recv[me] = hid_send[...]

        eye16 = eye(seqs)
        to_seq = dot_nt(eye16, to_slot).astype(BF16)
        act_f = act_row.astype(F32)
        live_col = jnp.sum(jnp.where(by_slot, jnp.broadcast_to(act_f, (seqs, seqs)), 0.0), axis=1, keepdims=True) > 0
        act_col = jnp.sum(
            jnp.where(iota((seqs, seqs), 0) == iota((seqs, seqs), 1), jnp.broadcast_to(act_f, (seqs, seqs)), 0.0),
            axis=1, keepdims=True,
        )
        live_row = jnp.sum(to_seq.astype(F32) * act_col, axis=0, keepdims=True) > 0
        eye_ch = eye(chans)
        g0 = norm_gain[...]
        g1 = g0.astype(BF16)
        r1 = g0 - g1.astype(F32)
        g2 = r1.astype(BF16)
        g3 = (r1 - g2.astype(F32)).astype(BF16)
        rows = jnp.concatenate([cx_w[...].astype(F32), cx_b[...].astype(F32), g1.astype(F32), g2.astype(F32), g3.astype(F32)], axis=0)
        cols = dot_nt(eye_ch, rows.astype(BF16))
        gain_col = (cols[:, 5:6] + cols[:, 6:7]) + cols[:, 7:8]
        brows = jnp.concatenate([cbc_w[...].astype(F32), cbc_b[...].astype(F32)], axis=0)
        bcols = dot_nt(eye(bc_dev), brows.astype(BF16))
        loads[3].wait()
        bc_old = [dot_nt(eye(bc_dev), cbcs[k]) for k in range(3)]
        bc_base = (bc_old[0] * bcols[:, 0:1] + bc_old[1] * bcols[:, 1:2]) + bc_old[2] * bcols[:, 2:3]
        loads[6].wait()
        x_old = [dot_nt(eye_ch, cxs[k]) for k in range(3)]
        x_base = (x_old[0] * cols[:, 0:1] + x_old[1] * cols[:, 1:2]) + x_old[2] * cols[:, 2:3]
        loads[7].wait()

        def narrow(b, carry):
            stb[b] = st[b].astype(BF16)
            return carry

        lax.fori_loop(0, seqs, narrow, 0)
        loads[0].wait()
        loads[1].wait()
        loads[2].wait()

        arrive(0, lambda who: hid_send, lambda who: hid_recv.at[who])
        parts = [None] * tiles
        for t in range(n_tp):
            at = (t * feats) // LANES
            for k in range(2):
                piece = hid_recv[t, k].astype(F32)
                parts[at + k] = piece if parts[at + k] is None else parts[at + k] + piece
        squares = parts[0] * parts[0]
        for k in range(1, tiles):
            squares = squares + parts[k] * parts[k]
        inv = lax.rsqrt(jnp.sum(squares, axis=1, keepdims=True) / width + EPS)
        for k in range(tiles):
            xn[:, k * LANES : (k + 1) * LANES] = (parts[k] * inv * gain[k : k + 1, :]).astype(BF16)

        bc_proj = dot_nt(bcw[...], xn[...]).astype(BF16)
        bc_conv = silu(bc_base + bc_proj.astype(F32) * bcols[:, 3:4] + bcols[:, 4:5]).astype(BF16)
        bc_send[...] = jnp.concatenate([bc_conv.astype(F32), jnp.zeros((bc_dev, LANES - seqs), F32)], axis=1).astype(BF16)
        bc_out = exchange(1, lambda peer: bc_send, lambda who: bc_recv.at[who], 0)
        bc_recv[me] = bc_send[...]

        dt_proj = dot_nt(dtw[...], xn[...]).astype(BF16).astype(F32)
        loads[5].wait()
        x_proj = dot_nt(xw[...], xn[...]).astype(BF16)
        loads[4].wait()
        z_proj = dot_nt(zw[...], xn[...]).astype(BF16)
        x_conv = silu(x_base + x_proj.astype(F32) * cols[:, 3:4] + cols[:, 4:5]).astype(BF16).astype(F32)
        z_gate = silu(z_proj.astype(F32))
        steps, decays, skips = [], [], []
        for h in range(heads):
            raw = dt_proj[h : h + 1, :] + dt_bias[h]
            step = jnp.maximum(raw, 0.0) + jnp.log1p(jnp.exp(-jnp.abs(raw)))
            rate = jnp.exp(jnp.full((1, seqs), log_rate[h], F32))
            decay = jnp.exp(-step * rate)
            steps.append(jnp.broadcast_to(jnp.where(live_row, step, 0.0), (HP, seqs)))
            decays.append(jnp.broadcast_to(jnp.where(live_row, decay, 1.0), (HP, seqs)))
            skips.append(jnp.full((HP, seqs), skip_gain[h], F32))
        dtx = jnp.concatenate(steps, axis=0) * x_conv
        decay = jnp.concatenate(decays, axis=0)
        skipped = jnp.concatenate(skips, axis=0) * x_conv
        x_now = dot_nt(eye16, x_proj)
        bc_now = dot_nt(eye16, bc_proj)
        for out, old, now in ((out_cx, cxs, x_now), (out_cbc, cbcs, bc_now)):
            held = [old[k].astype(F32) for k in range(3)]
            for k, new in enumerate((held[1], held[2], now)):
                out[k] = jnp.where(live_col, new, held[k]).astype(BF16)

        arrive(1, lambda who: bc_send, lambda who: bc_recv.at[who])
        groups = NS // bc_dev
        b_t = jnp.concatenate([bc_recv[t] for t in range(groups)], axis=0)[:, :seqs]
        c_t = jnp.concatenate([bc_recv[groups + t] for t in range(groups)], axis=0)[:, :seqs]
        b_f, c_f = b_t.astype(F32), c_t.astype(F32)
        bc_dot = jnp.sum(b_f * c_f, axis=0, keepdims=True)
        lane = iota((NS, seqs), 1)
        c_big = jnp.concatenate([jnp.where(lane == b, c_f, 0.0).astype(BF16) for b in range(seqs)], axis=0)
        s_big = jnp.concatenate([stb[b] for b in range(seqs)], axis=1)
        s_c = dot(s_big, c_big)
        y = (decay * s_c + dtx * bc_dot) + skipped
        gated = y * z_gate
        sq_send[...] = jnp.concatenate([jnp.sum(gated * gated, axis=0, keepdims=True), jnp.zeros((1, LANES - seqs), F32)], axis=1)
        sq_out = exchange(2, lambda peer: sq_send, lambda who: sq_recv.at[who], 0)
        scaled = (gated * gain_col).astype(BF16)
        loads[8].wait()
        rows_seq = dot_nt(to_seq, scaled).astype(BF16)
        branch = dot(rows_seq, ow[...])
        for k in range(tiles):
            br_send[k] = branch[:, k * LANES : (k + 1) * LANES].astype(BF16)

        def first_tile(who):
            return (who * feats) // LANES

        br_out = exchange(
            3, lambda peer: br_send.at[pl.ds(first_tile(peer), 2)], lambda who: br_recv.at[who], 0
        )
        br_recv[me] = br_send[pl.ds(first_tile(me), 2)]
        sq_recv[me] = sq_send[...]

        b_rows = dot_nt(eye16, b_t)
        for b in range(seqs):
            grown = dtx[:, b : b + 1] * b_rows[b : b + 1, :]
            st[b] = decay[:, b : b + 1] * st[b] + grown
        put = pltpu.make_async_copy(st, out_state, out_sem.at[0])
        put.start()

        arrive(2, lambda who: sq_send, lambda who: sq_recv.at[who])
        total_sq = sq_recv[0]
        for t in range(1, n_tp):
            total_sq = total_sq + sq_recv[t]
        sq_row = jnp.broadcast_to(total_sq[:, :seqs], (seqs, seqs))
        sq_col = jnp.sum(jnp.where(to_seq.astype(F32) > 0, sq_row, 0.0), axis=1, keepdims=True)
        inv_out = lax.rsqrt(sq_col / INNER + EPS)
        arrive(3, lambda who: br_send.at[pl.ds(0, 2)], lambda who: br_recv.at[who])
        sums = [br_recv[0, k].astype(F32) for k in range(2)]
        for t in range(1, n_tp):
            sums = [sums[k] + br_recv[t, k].astype(F32) for k in range(2)]
        whole = jnp.concatenate(sums, axis=1)
        branch_sum = pltpu.roll(whole, lax.rem(2 * LANES - shift, 2 * LANES), 1)[:, :feats]
        held = hid[...].astype(F32)
        fresh = (held + inv_out * branch_sum).astype(BF16).astype(F32)
        out_layer[...] = jnp.where(act_col > 0, fresh, held).astype(BF16)
        for copy in hid_out + bc_out + sq_out + br_out:
            copy.wait_send()
        put.wait()

    return body, offsets


def shards(
    hidden, in_gain, z_weight, x_weight, bc_weight, dt_weight, conv_x_weight, conv_x_bias,
    conv_bc_weight, conv_bc_bias, conv_x_state, conv_bc_state, dt_bias, log_rate, skip_gain,
    ssm_state, norm_gain, out_weight, pool_slot, active,
):
    n_tp = lax.axis_size("tp")
    seqs, feats = hidden.shape
    heads = ssm_state.shape[1]
    chans = z_weight.shape[1]
    bc_dev = bc_weight.shape[1]
    width = in_gain.shape[0]
    tiles = width // LANES
    body, offsets = make_kernel(n_tp, seqs, feats, heads, chans, bc_dev)
    vmem = pl.BlockSpec(memory_space=pltpu.VMEM)
    smem = pl.BlockSpec(memory_space=pltpu.SMEM)
    hbm = pl.BlockSpec(memory_space=pl.ANY)
    shape = jax.ShapeDtypeStruct
    out_layer, out_cx, out_cbc, out_state = pl.pallas_call(
        body,
        out_shape=(
            shape((seqs, feats), BF16),
            shape((3, seqs, chans), BF16),
            shape((3, seqs, bc_dev), BF16),
            shape((seqs, chans, NS), F32),
        ),
        in_specs=[
            vmem, vmem, vmem, hbm, hbm, hbm, hbm, hbm, vmem, vmem, vmem, vmem, hbm, hbm,
            smem, smem, smem, hbm, vmem, hbm,
        ],
        out_specs=(vmem, vmem, vmem, hbm),
        scratch_shapes=[
            pltpu.VMEM((chans, width), BF16),
            pltpu.VMEM((chans, width), BF16),
            pltpu.VMEM((bc_dev, width), BF16),
            pltpu.VMEM((heads, width), BF16),
            pltpu.VMEM((3, seqs, chans), BF16),
            pltpu.VMEM((3, seqs, bc_dev), BF16),
            pltpu.VMEM((seqs, chans, NS), F32),
            pltpu.VMEM((chans, width), BF16),
            pltpu.VMEM((tiles, LANES), F32),
            pltpu.VMEM((seqs, chans, NS), BF16),
            pltpu.VMEM((seqs, width), BF16),
            pltpu.VMEM((2, seqs, LANES), BF16),
            pltpu.VMEM((n_tp, 2, seqs, LANES), BF16),
            pltpu.VMEM((bc_dev, LANES), BF16),
            pltpu.VMEM((n_tp, bc_dev, LANES), BF16),
            pltpu.VMEM((1, LANES), F32),
            pltpu.VMEM((n_tp, 1, LANES), F32),
            pltpu.VMEM((tiles, seqs, LANES), BF16),
            pltpu.VMEM((n_tp, 2, seqs, LANES), BF16),
            pltpu.SemaphoreType.DMA((9,)),
            pltpu.SemaphoreType.DMA((1,)),
            pltpu.SemaphoreType.DMA((4, len(offsets))),
            pltpu.SemaphoreType.DMA((4, len(offsets))),
        ],
        compiler_params=pltpu.CompilerParams(
            collective_id=0, has_side_effects=True, vmem_limit_bytes=60 * 1024 * 1024
        ),
        name="step",
    )(
        hidden, pool_slot, active.reshape(1, seqs), in_gain.reshape(tiles, LANES),
        z_weight.T, x_weight.T, bc_weight.T, dt_weight.T,
        conv_x_weight, conv_x_bias.reshape(1, chans), conv_bc_weight, conv_bc_bias.reshape(1, bc_dev),
        conv_x_state.transpose(1, 0, 2), conv_bc_state.transpose(1, 0, 2),
        dt_bias, log_rate, skip_gain, ssm_state.reshape(seqs, chans, NS),
        norm_gain.reshape(1, chans), out_weight,
    )
    return (
        out_layer,
        out_cx.transpose(1, 0, 2),
        out_cbc.transpose(1, 0, 2),
        out_state.reshape(ssm_state.shape),
    )


def solution(mesh):
    rows = ("groups", "dp")
    placed = (
        P(rows, "tp"), P(), P(None, "tp"), P(None, "tp"), P(None, "tp"), P(None, "tp"), P(None, "tp"),
        P("tp"), P(None, "tp"), P("tp"), P(rows, None, "tp"), P(rows, None, "tp"), P("tp"), P("tp"),
        P("tp"), P(rows, "tp", None, None), P("tp"), P("tp", None), P(rows, None), P(rows),
    )
    return jax.shard_map(
        shards,
        mesh=mesh,
        in_specs=placed,
        out_specs=(P(rows, "tp"), P(rows, None, "tp"), P(rows, None, "tp"), P(rows, "tp", None, None)),
        check_vma=False,
    )
```

time: 95.4 us -> 54.1 us (0.57)
  Pallas kernels: 0 us -> 43.1 us
  starting transfers between devices: 39 us -> 0 us
  waiting for transfers between devices: 23.1 us -> 0 us
  other arithmetic: 12.7 us -> 0 us
  matrix products: 4.49 us -> 0 us
  local copies, waits for them, and re-layouts: 14.4 us -> 10 us
    pallas_call x0 -> x1, Pallas kernels: none -> 43.1 us  [shards(): pl.pallas_call(body, out_shape=(shape((seqs, feats), BF16), shape((3, seq...]
    all_to_all x4 -> x0, starting transfers between devices: 39 us -> none  [the longest x3 35 us: from_everyone(): lax.all_to_all(jnp.broadcast_to(x[None], (length, *x.shape)), axis, 0, 0,...]
    all_to_all x4 -> x0, waiting for transfers between devices: 23.1 us -> none  [the longest x3 11.8 us: from_everyone(): lax.all_to_all(jnp.broadcast_to(x[None], (length, *x.shape)), axis, 0, 0,...]
    unnamed x34 -> x4, local copies, waits for them, and re-layouts: 2.33 us -> 7.55 us
    select_n x6 -> x0, other arithmetic: 5.02 us -> none  [the longest x1 2.31 us: shards(): jnp.where(is_live[:, None, None, None], fresh_state, ssm_state)]
    dot_general x6 -> x0, matrix products: 4.49 us -> none  [the longest x4 3.1 us: shards(): jnp.dot(normed, matrix, preferred_element_type=jnp.float32)]
    convert_element_type x6 -> x0, other arithmetic: 4.15 us -> none  [the longest x2 1.94 us: convolve(): weight.astype(jnp.float32)[None]]
    gather x5 -> x0, local copies, waits for them, and re-layouts: 3.94 us -> none  [the longest x1 1.31 us: shards(): is_live = active[at_slot] > 0]
  transfers between devices with their start and end apart: 4 -> 0, of which waited for: 3 -> 0; matrix products, arithmetic and copies ran while one was open for 14% -> 0% of each run, Pallas kernels for 0% -> 0%
where the time goes in v1:
time: 54.1 us; the launch traced here: 53.8 us
  Pallas kernels  43.1 us (80%)
  local copies, waits for them, and re-layouts  10 us (18%)
  between operations  0.64 us (1%)
    pallas_call x1, Pallas kernels, shards(): pl.pallas_call(body, out_shape=(shape((seqs, feats), BF16), shape((3, seq...  43.1 us
    unnamed x4, local copies, waits for them, and re-layouts  7.55 us
    reshape x1, local copies, waits for them, and re-layouts, shards(): norm_gain.reshape(1, chans)  1.24 us
    reshape x1, local copies, waits for them, and re-layouts, shards(): conv_x_bias.reshape(1, chans)  1.24 us

profile of v1, /device:TPU:513, one launch (start us, length us, event | category | flops | bytes accessed | tf_op | source)
XLA Modules:
  0.0 53.8 jit_solution(15745633985904154452)
XLA Ops:
  0.6 1.2 %reshape.31.cx_b = bf16[1,320]{1,0:T(2,128)(2,1)} reshape(bf16[320]{0:T(512)(128)(2,1)} %param.27) | data formatting | bytes 1280 | tf_op jit(solution)/shard_map/reshape | solution.py:330
  1.9 1.2 %reshape.34.norm_gain = f32[1,320]{1,0:T(1,128)} reshape(f32[320]{0:T(512)} %param.36) | data formatting | bytes 2560 | tf_op jit(solution)/shard_map/reshape | solution.py:333
  3.1 43.1 %step.1 = (bf16[16,160]{1,0:T(8,128)(2,1)}, bf16[3,16,320]{2,1,0:T(8,128)(2,1)}, bf16[3,16,16]{2,1,0:T(8,128)(2,1)}, f32[16,320,128]{2,1,0:T(8,128)}) custom-call(bf16[16,160]{1,0:T(8,128)(2,1)} %hid.1, s32[1,16]{1,0:T(1,128)} %slot.1, s32[1,16]{1,0:T(1,128)} %bitcast.24, f32[20,128]{1,0:T(8,128)} %bitcast.22, bf16[320,2560]{1,0:T(8,128)(2,1)} %bitcast.15, ...), custom_call_target="tpu_custom_call" | custom-call | tf_op jit(solution)/shard_map/step/pallas_call | solution.py:285
  46.2 1.3 %copy.28 = bf16[16,160]{1,0:T(8,128)(2,1)} copy(bf16[16,160]{1,0:T(8,128)(2,1)} %get-tuple-element.16) | data formatting | bytes 10240
  47.5 1.4 %copy.29 = bf16[16,3,320]{2,0,1:T(8,128)(2,1)} copy(bf16[16,3,320]{2,0,1:T(8,128)(2,1)} %bitcast.20) | data formatting | bytes 61440
  48.9 1.3 %copy.30 = bf16[16,3,16]{2,0,1:T(8,128)(2,1)} copy(bf16[16,3,16]{2,0,1:T(8,128)(2,1)} %bitcast.21) | data formatting | bytes 3072
  50.2 3.6 %copy.31 = f32[16,5,64,128]{3,2,1,0:T(8,128)} copy(f32[16,5,64,128]{3,2,1,0:T(8,128)} %bitcast.14) | data formatting | bytes 5242880

commit v2 on v1

--- a/solution.py
+++ b/solution.py
@@ -34,6 +34,15 @@
 
 def silu(x):
     return x * jax.nn.sigmoid(x)
+
+
+def put_out(*refs):
+    sems = refs[-1]
+    copies = [pltpu.make_async_copy(refs[k], refs[4 + k], sems.at[k]) for k in (3, 0, 1, 2)]
+    for copy in copies:
+        copy.start()
+    for copy in copies:
+        copy.wait()
 
 
 def make_kernel(n_tp, seqs, feats, heads, chans, bc_dev):
@@ -54,7 +63,7 @@
         out_layer, out_cx, out_cbc, out_state,
         zw, xw, bcw, dtw, cxs, cbcs, st, ow, gain, stb, xn,
         hid_send, hid_recv, bc_send, bc_recv, sq_send, sq_recv, br_send, br_recv,
-        in_sem, out_sem, send_sem, recv_sem,
+        in_sem, send_sem, recv_sem,
     ):
         me = lax.axis_index("tp")
         chip, core = me // 2, lax.rem(me, 2)
@@ -132,12 +141,12 @@
         )
         live_row = jnp.sum(to_seq.astype(F32) * act_col, axis=0, keepdims=True) > 0
         eye_ch = eye(chans)
-        g0 = norm_gain[...]
+        g0 = norm_gain[...].reshape(1, chans)
         g1 = g0.astype(BF16)
         r1 = g0 - g1.astype(F32)
         g2 = r1.astype(BF16)
         g3 = (r1 - g2.astype(F32)).astype(BF16)
-        rows = jnp.concatenate([cx_w[...].astype(F32), cx_b[...].astype(F32), g1.astype(F32), g2.astype(F32), g3.astype(F32)], axis=0)
+        rows = jnp.concatenate([cx_w[...].astype(F32), cx_b[...].astype(F32).reshape(1, chans), g1.astype(F32), g2.astype(F32), g3.astype(F32)], axis=0)
         cols = dot_nt(eye_ch, rows.astype(BF16))
         gain_col = (cols[:, 5:6] + cols[:, 6:7]) + cols[:, 7:8]
         brows = jnp.concatenate([cbc_w[...].astype(F32), cbc_b[...].astype(F32)], axis=0)
@@ -238,9 +247,7 @@
         b_rows = dot_nt(eye16, b_t)
         for b in range(seqs):
             grown = dtx[:, b : b + 1] * b_rows[b : b + 1, :]
-            st[b] = decay[:, b : b + 1] * st[b] + grown
-        put = pltpu.make_async_copy(st, out_state, out_sem.at[0])
-        put.start()
+            out_state[b] = decay[:, b : b + 1] * st[b] + grown
 
         arrive(2, lambda who: sq_send, lambda who: sq_recv.at[who])
         total_sq = sq_recv[0]
@@ -260,7 +267,6 @@
         out_layer[...] = jnp.where(act_col > 0, fresh, held).astype(BF16)
         for copy in hid_out + bc_out + sq_out + br_out:
             copy.wait_send()
-        put.wait()
 
     return body, offsets
 
@@ -282,19 +288,20 @@
     smem = pl.BlockSpec(memory_space=pltpu.SMEM)
     hbm = pl.BlockSpec(memory_space=pl.ANY)
     shape = jax.ShapeDtypeStruct
-    out_layer, out_cx, out_cbc, out_state = pl.pallas_call(
+    results = (
+        ((seqs, feats), BF16),
+        ((3, seqs, chans), BF16),
+        ((3, seqs, bc_dev), BF16),
+        ((seqs, chans, NS), F32),
+    )
+    made = pl.pallas_call(
         body,
-        out_shape=(
-            shape((seqs, feats), BF16),
-            shape((3, seqs, chans), BF16),
-            shape((3, seqs, bc_dev), BF16),
-            shape((seqs, chans, NS), F32),
-        ),
+        out_shape=tuple(pltpu.VMEM(dims, kind) for dims, kind in results),
         in_specs=[
             vmem, vmem, vmem, hbm, hbm, hbm, hbm, hbm, vmem, vmem, vmem, vmem, hbm, hbm,
             smem, smem, smem, hbm, vmem, hbm,
         ],
-        out_specs=(vmem, vmem, vmem, hbm),
+        out_specs=(vmem,) * 4,
         scratch_shapes=[
             pltpu.VMEM((chans, width), BF16),
             pltpu.VMEM((chans, width), BF16),
@@ -316,7 +323,6 @@
             pltpu.VMEM((tiles, seqs, LANES), BF16),
             pltpu.VMEM((n_tp, 2, seqs, LANES), BF16),
             pltpu.SemaphoreType.DMA((9,)),
-            pltpu.SemaphoreType.DMA((1,)),
             pltpu.SemaphoreType.DMA((4, len(offsets))),
             pltpu.SemaphoreType.DMA((4, len(offsets))),
         ],
@@ -327,11 +333,19 @@
     )(
         hidden, pool_slot, active.reshape(1, seqs), in_gain.reshape(tiles, LANES),
         z_weight.T, x_weight.T, bc_weight.T, dt_weight.T,
-        conv_x_weight, conv_x_bias.reshape(1, chans), conv_bc_weight, conv_bc_bias.reshape(1, bc_dev),
+        conv_x_weight, conv_x_bias, conv_bc_weight, conv_bc_bias.reshape(1, bc_dev),
         conv_x_state.transpose(1, 0, 2), conv_bc_state.transpose(1, 0, 2),
         dt_bias, log_rate, skip_gain, ssm_state.reshape(seqs, chans, NS),
-        norm_gain.reshape(1, chans), out_weight,
-    )
+        norm_gain, out_weight,
+    )
+    out_layer, out_cx, out_cbc, out_state = pl.pallas_call(
+        put_out,
+        out_shape=tuple(shape(dims, kind) for dims, kind in results),
+        in_specs=[vmem] * 4,
+        out_specs=(hbm,) * 4,
+        scratch_shapes=[pltpu.SemaphoreType.DMA((4,))],
+        name="put",
+    )(*(pltpu.with_memory_space_constraint(x, pltpu.VMEM) for x in made))
     return (
         out_layer,
         out_cx.transpose(1, 0, 2),

time: 54.1 us -> 44.9 us (0.83)
  local copies, waits for them, and re-layouts: 10 us -> 0 us
  Pallas kernels: 43.1 us -> 44.1 us
    unnamed x4 -> x0, local copies, waits for them, and re-layouts: 7.55 us -> none
    reshape x2 -> x0, local copies, waits for them, and re-layouts: 2.49 us -> none  [the longest x1 1.24 us: shards(): norm_gain.reshape(1, chans)]
    pallas_call x1 -> x2, Pallas kernels: 43.1 us -> 44.1 us  [the longest x1 42.6 us: shards(): pl.pallas_call(body, out_shape=tuple((pltpu.VMEM(dims, kind) for dims, ki...]
where the time goes in v2:
time: 44.9 us; the launch traced here: 44.8 us
  Pallas kernels  44.1 us (98%)
  between operations  0.65 us (1%)
    pallas_call x1, Pallas kernels, shards(): pl.pallas_call(body, out_shape=tuple((pltpu.VMEM(dims, kind) for dims, ki...  42.6 us
    pallas_call x1, Pallas kernels, shards(): pl.pallas_call(put_out, out_shape=tuple((shape(dims, kind) for dims, kind...  1.53 us

profile of v2, /device:TPU:513, one launch (start us, length us, event | category | flops | bytes accessed | tf_op | source)
XLA Modules:
  0.0 44.8 jit_solution(7760818952409213564)
XLA Ops:
  0.6 42.6 %step.1 = (bf16[16,160]{1,0:T(8,128)(2,1)S(1)}, bf16[3,16,320]{2,1,0:T(8,128)(2,1)S(1)}, bf16[3,16,16]{2,1,0:T(8,128)(2,1)S(1)}, f32[16,320,128]{2,1,0:T(8,128)S(1)}) custom-call(bf16[16,160]{1,0:T(8,128)(2,1)} %hid.1, s32[1,16]{1,0:T(1,128)} %slot.1, s32[1,16]{1,0:T(1,128)} %bitcast.21, f32[20,128]{1,0:T(8,128)} %bitcast.19, bf16[320,2560]{1,0:T(8,128)(2,1)} %bitcast.14, ...), custom_call_target="tpu_custom_call" | custom-call | tf_op jit(solution)/shard_map/step/pallas_call | solution.py:297
  43.2 1.5 %put.1 = (bf16[16,160]{1,0:T(8,128)(2,1)}, bf16[3,16,320]{2,1,0:T(8,128)(2,1)}, bf16[3,16,16]{2,1,0:T(8,128)(2,1)}, f32[16,320,128]{2,1,0:T(8,128)}) custom-call(bf16[16,160]{1,0:T(8,128)(2,1)S(1)} %get-tuple-element.12.refs_0_, bf16[3,16,320]{2,1,0:T(8,128)(2,1)S(1)} %get-tuple-element.13.refs_1_, bf16[3,16,16]{2,1,0:T(8,128)(2,1)S(1)} %get-tuple-element.14.refs_2_, ...), custom_call_target="tpu_custom_call" | custom-call | tf_op jit(solution)/shard_map/put/pallas_call | solution.py:341

commit v3 on v2

v3 whole, which is shorter than its diff:
```python
import jax
import jax.numpy as jnp
from jax import lax
from jax.experimental import pallas as pl
from jax.experimental.pallas import tpu as pltpu
from jax.sharding import PartitionSpec as P

HP = 64
NS = 128
INNER = 5120
EPS = 1e-05
F32 = jnp.float32
BF16 = jnp.bfloat16
LANES = 128
SUBS = 8

NT = (((1,), (1,)), ((), ()))
MESH = pl.DeviceIdType.MESH


def dot(a, b):
    return jnp.dot(a, b, preferred_element_type=F32)


def dot_nt(a, b):
    return lax.dot_general(a, b, NT, preferred_element_type=F32)


def iota(shape, dim):
    return lax.broadcasted_iota(jnp.int32, shape, dim)


def one_hot(mask):
    return mask.astype(F32).astype(BF16)


def eye(n):
    return one_hot(iota((n, n), 0) == iota((n, n), 1))


def silu(x):
    return x * jax.nn.sigmoid(x)


def exact_dot(x, picks):
    first = x.astype(BF16)
    rest = x - first.astype(F32)
    second = rest.astype(BF16)
    third = (rest - second.astype(F32)).astype(BF16)
    return (dot(first, picks) + dot(second, picks)) + dot(third, picks)


def put_out(*refs):
    sems = refs[-1]
    copies = [pltpu.make_async_copy(refs[k], refs[4 + k], sems.at[k]) for k in (3, 0, 1, 2)]
    for copy in copies:
        copy.start()
    for copy in copies:
        copy.wait()


def make_kernel(n_tp, seqs, feats, heads, chans, bc_dev):
    width = n_tp * feats
    tiles = width // LANES
    chips = n_tp // 2
    half = chips // 2
    steps_far = [half]
    for far in range(half - 1, 0, -1):
        steps_far += [far, chips - far]
    partners = [(step, flip) for step in steps_far for flip in (1, 0)] + [(0, 1)]
    others = len(partners)

    def body(
        hid, slot, act, in_gain, z_w, x_w, bc_w, dt_w, cx_w, cx_b, cbc_w, cbc_b, cx_s, cbc_s,
        dt_bias, log_rate, skip_gain, state, norm_gain, out_w,
        out_layer, out_cx, out_cbc, out_state,
        zw, xw, bcw, dtw, cxs, cbcs, st, ow, gain, slot_v, slot_m, act_v, cxw, cxb, cbcw, cbcb, ngain,
        dtb_m, rate_m, skip_m,
        stb, xn, hid_recv, bc_send, bc_recv, sq_send, sq_recv, br_send, br_recv,
        in_sem, send_sem, recv_sem, relay_sem,
    ):
        me = lax.axis_index("tp")
        chip, core = me // 2, lax.rem(me, 2)
        barrier = pltpu.get_barrier_semaphore()

        def device(step, which):
            return {"tp": lax.rem(chip + step, chips) * 2 + which}

        loads = {}

        def load(name, src, dst):
            loads[name] = pltpu.make_async_copy(src, dst, in_sem.at[len(loads)])
            loads[name].start()

        load("hid", hid, hid_recv.at[core])

        @pl.when(core == 0)
        def _():
            pl.semaphore_signal(barrier, inc=1, device_id=device(0, 1), device_id_type=MESH)

        @pl.when(core == 1)
        def _():
            for step in steps_far:
                pl.semaphore_signal(barrier, inc=1, device_id=device(step, 1), device_id_type=MESH)

        load("slot", slot, slot_v)
        load("slot_m", slot, slot_m)
        load("act", act, act_v)
        load("bc_w", bc_w, bcw)
        load("in_gain", in_gain, gain)
        load("cbc_s", cbc_s, cbcs)
        load("cbc_w", cbc_w, cbcw)
        load("cbc_b", cbc_b, cbcb)
        load("dt_w", dt_w, dtw)
        load("cx_s", cx_s, cxs)
        load("cx_w", cx_w, cxw)
        load("cx_b", cx_b, cxb)
        load("norm_gain", norm_gain, ngain)
        load("dt_bias", dt_bias, dtb_m)
        load("log_rate", log_rate, rate_m)
        load("skip_gain", skip_gain, skip_m)
        load("state", state, st)
        load("x_w", x_w, xw)
        load("z_w", z_w, zw)
        load("out_w", out_w, ow)

        def first_send(step, which, dst_slot):
            return pltpu.make_async_remote_copy(
                src_ref=hid_recv.at[core], dst_ref=hid_recv.at[dst_slot],
                send_sem=send_sem.at[0], recv_sem=recv_sem.at[0],
                device_id=device(step, which), device_id_type=MESH,
            )

        def relay():
            return pltpu.make_async_remote_copy(
                src_ref=hid_recv.at[pl.ds(1, n_tp - 1)], dst_ref=hid_recv.at[pl.ds(1, n_tp - 1)],
                send_sem=relay_sem.at[0], recv_sem=recv_sem.at[0],
                device_id=device(0, 0), device_id_type=MESH,
            )

        @pl.when(core == 0)
        def _():
            loads["hid"].wait()
            pl.semaphore_wait(barrier, 1)
            for step in steps_far:
                first_send(step, 1, 2 * (chips - step)).start()
            first_send(0, 1, 0).start()

        @pl.when(core == 1)
        def _():
            loads["hid"].wait()
            pl.semaphore_wait(barrier, chips)
            pl.semaphore_signal(barrier, inc=1, device_id=device(0, 0), device_id_type=MESH)
            for step in steps_far:
                first_send(step, 1, 2 * (chips - step) + 1).start()

        for name in ("slot", "slot_m", "act", "in_gain", "cbc_s", "cbc_w", "cbc_b"):
            loads[name].wait()
        slot_row = slot_v[...]
        by_slot = iota((seqs, seqs), 0) == jnp.broadcast_to(slot_row, (seqs, seqs))
        to_slot = one_hot(by_slot)
        eye16 = eye(seqs)
        diagonal = iota((seqs, seqs), 0) == iota((seqs, seqs), 1)
        to_seq = dot_nt(eye16, to_slot).astype(BF16)
        act_f = jnp.broadcast_to(act_v[...].astype(F32), (seqs, seqs))
        live_row = act_v[...] > 0
        act_col = jnp.sum(jnp.where(diagonal, act_f, 0.0), axis=1, keepdims=True) > 0
        live_slot = jnp.sum(jnp.where(by_slot, act_f, 0.0), axis=1, keepdims=True) > 0
        bc_rows = jnp.concatenate([cbcw[...].astype(F32), cbcb[...].astype(F32)], axis=0)
        row_at, col_at = iota((bc_dev, bc_dev), 0), iota((bc_dev, bc_dev), 1)
        mirror = one_hot(col_at == row_at // SUBS * SUBS + lax.rem(SUBS - lax.rem(row_at, SUBS), SUBS))
        bc_cols = dot_nt(mirror, bc_rows.astype(BF16))
        bc_old = [dot_nt(mirror, dot(to_seq, cbcs[k]).astype(BF16)) for k in range(3)]
        bc_base = (bc_old[0] * bc_cols[:, 0:1] + bc_old[1] * bc_cols[:, 1:2]) + bc_old[2] * bc_cols[:, 2:3]
        for name in ("cx_s", "cx_w", "cx_b", "norm_gain", "dt_bias", "log_rate", "skip_gain"):
            loads[name].wait()
        eye_ch = eye(chans)
        g0 = ngain[...].reshape(1, chans)
        g1 = g0.astype(BF16).astype(F32)
        g2 = (g0 - g1).astype(BF16).astype(F32)
        g3 = (g0 - g1) - g2
        rows = jnp.concatenate([cxw[...].astype(F32), cxb[...].astype(F32).reshape(1, chans), g1, g2, g3], axis=0)
        cols = dot_nt(eye_ch, rows.astype(BF16))
        gain_col = (cols[:, 5:6] + cols[:, 6:7]) + cols[:, 7:8]
        x_old = [dot_nt(eye_ch, dot(to_seq, cxs[k]).astype(BF16)) for k in range(3)]
        x_base = (x_old[0] * cols[:, 0:1] + x_old[1] * cols[:, 1:2]) + x_old[2] * cols[:, 2:3]
        loads["state"].wait()

        def narrow(i, carry):
            stb[i] = st[slot_m[0, i]].astype(BF16)
            return carry

        lax.fori_loop(0, seqs, narrow, 0)
        for name in ("bc_w", "dt_w"):
            loads[name].wait()
        bcw[...] = dot(mirror, bcw[...]).astype(BF16)

        pltpu.make_async_remote_copy(
            src_ref=hid_recv.at[pl.ds(1, n_tp - 1)], dst_ref=hid_recv.at[pl.ds(1, n_tp - 1)],
            send_sem=send_sem.at[0], recv_sem=recv_sem.at[0],
            device_id=device(0, 1 - core), device_id_type=MESH,
        ).wait_recv()

        @pl.when(core == 1)
        def _():
            relay().start()

        blocks = [
            hid_recv[2 * lax.rem(t // 2 - chip + chips, chips) + t % 2].astype(F32) for t in range(n_tp)
        ]
        whole = jnp.concatenate(blocks, axis=1)
        squares = whole[:, :LANES] * whole[:, :LANES]
        for k in range(1, tiles):
            part = whole[:, k * LANES : (k + 1) * LANES]
            squares = squares + part * part
        inv = lax.rsqrt(jnp.sum(squares, axis=1, keepdims=True) / width + EPS)
        for k in range(tiles):
            at = slice(k * LANES, (k + 1) * LANES)
            xn[:, at] = (whole[:, at] * inv * gain[k : k + 1, :]).astype(BF16)

        bc_proj = dot_nt(bcw[...], xn[...]).astype(BF16)
        bc_conv = silu(bc_base + bc_proj.astype(F32) * bc_cols[:, 3:4] + bc_cols[:, 4:5]).astype(BF16).astype(F32)
        spread = jnp.concatenate([bc_conv, jnp.zeros((bc_dev, LANES - seqs), F32)], axis=1)
        spread = pltpu.roll(spread, 0, 1, stride=seqs, stride_axis=0)
        bc_send[...] = jnp.sum(spread.reshape(bc_dev // SUBS, SUBS, LANES), axis=1)

        def exchange(phase, src_of, dst_ref):
            for step, flip in partners:
                peer = lax.rem(chip + step, chips) * 2 + (lax.rem(core + 1, 2) if flip else core)
                pltpu.make_async_remote_copy(
                    src_ref=src_of(peer), dst_ref=dst_ref.at[me],
                    send_sem=send_sem.at[phase], recv_sem=recv_sem.at[phase],
                    device_id={"tp": peer}, device_id_type=MESH,
                ).start()

        def all_of(phase, dst_ref):
            return pltpu.make_async_remote_copy(
                src_ref=dst_ref.at[pl.ds(0, others)], dst_ref=dst_ref.at[pl.ds(0, others)],
                send_sem=send_sem.at[phase], recv_sem=recv_sem.at[phase],
                device_id=device(0, 1 - core), device_id_type=MESH,
            )

        exchange(1, lambda peer: bc_send, bc_recv)
        bc_recv[me] = bc_send[...]

        dt_proj = dot_nt(dtw[...], xn[...]).astype(BF16).astype(F32)
        loads["x_w"].wait()
        x_proj = dot_nt(xw[...], xn[...]).astype(BF16)
        loads["z_w"].wait()
        z_proj = dot_nt(zw[...], xn[...]).astype(BF16)
        x_conv = silu(x_base + x_proj.astype(F32) * cols[:, 3:4] + cols[:, 4:5]).astype(BF16)
        x_f = x_conv.astype(F32)
        z_gate = silu(z_proj.astype(F32))
        steps, decays = [], []
        for h in range(heads):
            raw = dt_proj[h : h + 1, :] + dtb_m[h]
            step = jnp.maximum(raw, 0.0) + jnp.log1p(jnp.exp(-jnp.abs(raw)))
            rate = jnp.exp(jnp.full((1, seqs), rate_m[h], F32))
            steps.append(jnp.where(live_row, step, 0.0))
            decays.append(jnp.where(live_row, jnp.exp(-step * rate), 1.0))

        def per_channel(values):
            return jnp.concatenate([jnp.broadcast_to(v, (HP, seqs)) for v in values], axis=0)

        dtx = per_channel(steps) * x_f
        decay = per_channel(decays)
        skipped = jnp.concatenate([jnp.full((HP, seqs), skip_m[h], F32) for h in range(heads)], axis=0) * x_f

        all_of(1, bc_recv).wait_recv()

        def unpacked(at):
            found = []
            for row in range(NS // SUBS):
                line = at // SUBS + row
                packed = bc_recv[line // (bc_dev // SUBS), pl.ds(line % (bc_dev // SUBS), 1), :]
                found.append(
                    pltpu.roll(jnp.broadcast_to(packed, (SUBS, LANES)), 0, 1, stride=seqs, stride_axis=0)
                )
            return jnp.concatenate(found, axis=0)[:, :seqs]

        c_f, b_f = unpacked(NS), unpacked(0)
        lane = iota((NS, seqs), 1)
        c_big = jnp.concatenate([jnp.where(lane == b, c_f, 0.0).astype(BF16) for b in range(seqs)], axis=0)
        s_big = jnp.concatenate([stb[b] for b in range(seqs)], axis=1)
        s_c = dot(s_big, c_big)
        bc_dot = jnp.sum(b_f * c_f, axis=0, keepdims=True)
        y = (decay * s_c + dtx * bc_dot) + skipped
        gated = y * z_gate
        scaled = (gated * gain_col).astype(BF16)
        sq_send[...] = jnp.concatenate(
            [jnp.sum(gated * gated, axis=0, keepdims=True), jnp.zeros((1, LANES - seqs), F32)], axis=1
        )
        exchange(2, lambda peer: sq_send, sq_recv)
        loads["out_w"].wait()
        branch = dot(dot_nt(eye16, scaled).astype(BF16), ow[...])
        for k in range(tiles):
            br_send[k] = branch[:, k * LANES : (k + 1) * LANES].astype(BF16)

        def first_tile(who):
            return (who * feats) // LANES

        exchange(3, lambda peer: br_send.at[pl.ds(first_tile(peer), 2)], br_recv)
        br_recv[me] = br_send[pl.ds(first_tile(me), 2)]
        sq_recv[me] = sq_send[...]

        x_now = dot_nt(to_slot, x_proj)
        bc_now = dot(dot_nt(to_slot, bc_proj).astype(BF16), mirror)
        for out, old, now in ((out_cx, cxs, x_now), (out_cbc, cbcs, bc_now)):
            held = [old[k].astype(F32) for k in range(3)]
            for k, new in enumerate((held[1], held[2], now)):
                out[k] = jnp.where(live_slot, new, held[k]).astype(BF16)
        of_heads = jnp.concatenate(steps + decays + [jnp.zeros((-2 * heads % SUBS, seqs), F32)], axis=0)
        of_heads = exact_dot(of_heads, to_seq)
        steps_slot = [of_heads[h : h + 1, :] for h in range(heads)]
        decays_slot = [of_heads[heads + h : heads + h + 1, :] for h in range(heads)]
        dtx_slot = per_channel(steps_slot) * dot(x_conv, to_seq)
        decay_slot = per_channel(decays_slot)
        b_rows = dot_nt(to_slot, b_f.astype(BF16))
        for b in range(seqs):
            grown = dtx_slot[:, b : b + 1] * b_rows[b : b + 1, :]
            out_state[b] = decay_slot[:, b : b + 1] * st[b] + grown

        all_of(2, sq_recv).wait_recv()
        total_sq = sq_recv[0]
        for t in range(1, n_tp):
            total_sq = total_sq + sq_recv[t]
        sq_all = jnp.broadcast_to(total_sq[:, :seqs], (seqs, seqs))
        sq_col = jnp.sum(jnp.where(diagonal, sq_all, 0.0), axis=1, keepdims=True)
        inv_out = lax.rsqrt(sq_col / INNER + EPS)
        all_of(3, br_recv).wait_recv()
        sums = [br_recv[0, k].astype(F32) for k in range(2)]
        for t in range(1, n_tp):
            sums = [sums[k] + br_recv[t, k].astype(F32) for k in range(2)]
        shift = lax.rem(me * feats, LANES)
        branch_sum = pltpu.roll(jnp.concatenate(sums, axis=1), lax.rem(2 * LANES - shift, 2 * LANES), 1)[:, :feats]
        kept = hid_recv[core].astype(F32)
        fresh = (kept + inv_out * branch_sum).astype(BF16).astype(F32)
        out_layer[...] = jnp.where(act_col, fresh, kept).astype(BF16)

        for phase, ref in ((1, bc_recv), (2, sq_recv), (3, br_recv)):
            all_of(phase, ref).wait_send()

        def hid_sent(count):
            return pltpu.make_async_remote_copy(
                src_ref=hid_recv.at[pl.ds(0, count)], dst_ref=hid_recv.at[pl.ds(0, count)],
                send_sem=send_sem.at[0], recv_sem=recv_sem.at[0],
                device_id=device(0, 1 - core), device_id_type=MESH,
            )

        @pl.when(core == 0)
        def _():
            hid_sent(chips).wait_send()

        @pl.when(core == 1)
        def _():
            hid_sent(chips - 1).wait_send()
            relay().wait_send()

    return body


def shards(
    hidden, in_gain, z_weight, x_weight, bc_weight, dt_weight, conv_x_weight, conv_x_bias,
    conv_bc_weight, conv_bc_bias, conv_x_state, conv_bc_state, dt_bias, log_rate, skip_gain,
    ssm_state, norm_gain, out_weight, pool_slot, active,
):
    n_tp = lax.axis_size("tp")
    seqs, feats = hidden.shape
    heads = ssm_state.shape[1]
    chans = z_weight.shape[1]
    bc_dev = bc_weight.shape[1]
    width = in_gain.shape[0]
    tiles = width // LANES
    vmem = pl.BlockSpec(memory_space=pltpu.VMEM)
    hbm = pl.BlockSpec(memory_space=pl.ANY)
    shape = jax.ShapeDtypeStruct
    results = (
        ((seqs, feats), BF16),
        ((3, seqs, chans), BF16),
        ((3, seqs, bc_dev), BF16),
        ((seqs, chans, NS), F32),
    )
    made = pl.pallas_call(
        make_kernel(n_tp, seqs, feats, heads, chans, bc_dev),
        out_shape=tuple(pltpu.VMEM(dims, kind) for dims, kind in results),
        in_specs=[hbm] * 20,
        out_specs=(vmem,) * 4,
        scratch_shapes=[
            pltpu.VMEM((chans, width), BF16),
            pltpu.VMEM((chans, width), BF16),
            pltpu.VMEM((bc_dev, width), BF16),
            pltpu.VMEM((heads, width), BF16),
            pltpu.VMEM((3, seqs, chans), BF16),
            pltpu.VMEM((3, seqs, bc_dev), BF16),
            pltpu.VMEM((seqs, chans, NS), F32),
            pltpu.VMEM((chans, width), BF16),
            pltpu.VMEM((tiles, LANES), F32),
            pltpu.VMEM((1, seqs), jnp.int32),
            pltpu.SMEM((1, seqs), jnp.int32),
            pltpu.VMEM((1, seqs), jnp.int32),
            pltpu.VMEM((4, chans), BF16),
            pltpu.VMEM((chans,), BF16),
            pltpu.VMEM((4, bc_dev), BF16),
            pltpu.VMEM((1, bc_dev), BF16),
            pltpu.VMEM((chans,), F32),
            pltpu.SMEM((heads,), F32),
            pltpu.SMEM((heads,), F32),
            pltpu.SMEM((heads,), F32),
            pltpu.VMEM((seqs, chans, NS), BF16),
            pltpu.VMEM((seqs, width), BF16),
            pltpu.VMEM((n_tp, seqs, feats), BF16),
            pltpu.VMEM((bc_dev // SUBS, LANES), F32),
            pltpu.VMEM((n_tp, bc_dev // SUBS, LANES), F32),
            pltpu.VMEM((1, LANES), F32),
            pltpu.VMEM((n_tp, 1, LANES), F32),
            pltpu.VMEM((tiles, seqs, LANES), BF16),
            pltpu.VMEM((n_tp, 2, seqs, LANES), BF16),
            pltpu.SemaphoreType.DMA((21,)),
            pltpu.SemaphoreType.DMA((4,)),
            pltpu.SemaphoreType.DMA((4,)),
            pltpu.SemaphoreType.DMA((1,)),
        ],
        compiler_params=pltpu.CompilerParams(
            collective_id=0, has_side_effects=True, vmem_limit_bytes=60 * 1024 * 1024
        ),
        name="step",
    )(
        hidden, pool_slot, active.reshape(1, seqs), in_gain.reshape(tiles, LANES),
        z_weight.T, x_weight.T, bc_weight.T, dt_weight.T,
        conv_x_weight, conv_x_bias, conv_bc_weight, conv_bc_bias.reshape(1, bc_dev),
        conv_x_state.transpose(1, 0, 2), conv_bc_state.transpose(1, 0, 2),
        dt_bias, log_rate, skip_gain, ssm_state.reshape(seqs, chans, NS),
        norm_gain, out_weight,
    )
    out_layer, out_cx, out_cbc, out_state = pl.pallas_call(
        put_out,
        out_shape=tuple(shape(dims, kind) for dims, kind in results),
        in_specs=[vmem] * 4,
        out_specs=(hbm,) * 4,
        scratch_shapes=[pltpu.SemaphoreType.DMA((4,))],
        name="put",
    )(*(pltpu.with_memory_space_constraint(x, pltpu.VMEM) for x in made))
    return (
        out_layer,
        out_cx.transpose(1, 0, 2),
        out_cbc.transpose(1, 0, 2),
        out_state.reshape(ssm_state.shape),
    )


def solution(mesh):
    rows = ("groups", "dp")
    placed = (
        P(rows, "tp"), P(), P(None, "tp"), P(None, "tp"), P(None, "tp"), P(None, "tp"), P(None, "tp"),
        P("tp"), P(None, "tp"), P("tp"), P(rows, None, "tp"), P(rows, None, "tp"), P("tp"), P("tp"),
        P("tp"), P(rows, "tp", None, None), P("tp"), P("tp", None), P(rows, None), P(rows),
    )
    return jax.shard_map(
        shards,
        mesh=mesh,
        in_specs=placed,
        out_specs=(P(rows, "tp"), P(rows, None, "tp"), P(rows, None, "tp"), P(rows, "tp", None, None)),
        check_vma=False,
    )
```

time: 44.9 us -> 39.9 us (0.89)
  Pallas kernels: 44.1 us -> 39.1 us
    pallas_call x1, Pallas kernels: 42.6 us -> 37.6 us  [shards(): pl.pallas_call(make_kernel(n_tp, seqs, feats, heads, chans, bc_dev), out_...]
where the time goes in v3:
time: 39.9 us; the launch traced here: 39.7 us
  Pallas kernels  39.1 us (98%)
  between operations  0.65 us (2%)
    pallas_call x1, Pallas kernels, shards(): pl.pallas_call(make_kernel(n_tp, seqs, feats, heads, chans, bc_dev), out_...  37.6 us
    pallas_call x1, Pallas kernels, shards(): pl.pallas_call(put_out, out_shape=tuple((shape(dims, kind) for dims, kind...  1.53 us

profile of v3, /device:TPU:513, one launch (start us, length us, event | category | flops | bytes accessed | tf_op | source)
XLA Modules:
  0.0 39.7 jit_solution(5887439283440050257)
XLA Ops:
  0.6 37.6 %step.1 = (bf16[16,160]{1,0:T(8,128)(2,1)S(1)}, bf16[3,16,320]{2,1,0:T(8,128)(2,1)S(1)}, bf16[3,16,16]{2,1,0:T(8,128)(2,1)S(1)}, f32[16,320,128]{2,1,0:T(8,128)S(1)}) custom-call(bf16[16,160]{1,0:T(8,128)(2,1)} %hid.1, s32[1,16]{1,0:T(1,128)} %slot.1, s32[1,16]{1,0:T(1,128)} %bitcast.21, f32[20,128]{1,0:T(8,128)} %bitcast.19, bf16[320,2560]{1,0:T(8,128)(2,1)} %bitcast.14, ...), custom_call_target="tpu_custom_call" | custom-call | tf_op jit(solution)/shard_map/step/pallas_call | solution.py:383
  38.2 1.5 %put.1 = (bf16[16,160]{1,0:T(8,128)(2,1)}, bf16[3,16,320]{2,1,0:T(8,128)(2,1)}, bf16[3,16,16]{2,1,0:T(8,128)(2,1)}, f32[16,320,128]{2,1,0:T(8,128)}) custom-call(bf16[16,160]{1,0:T(8,128)(2,1)S(1)} %get-tuple-element.12.refs_0_, bf16[3,16,320]{2,1,0:T(8,128)(2,1)S(1)} %get-tuple-element.13.refs_1_, bf16[3,16,16]{2,1,0:T(8,128)(2,1)S(1)} %get-tuple-element.14.refs_2_, ...), custom_call_target="tpu_custom_call" | custom-call | tf_op jit(solution)/shard_map/put/pallas_call | solution.py:435

commit v4 on v3

--- a/solution.py
+++ b/solution.py
@@ -67,8 +67,7 @@
     steps_far = [half]
     for far in range(half - 1, 0, -1):
         steps_far += [far, chips - far]
-    partners = [(step, flip) for step in steps_far for flip in (1, 0)] + [(0, 1)]
-    others = len(partners)
+    others = n_tp - 1
 
     def body(
         hid, slot, act, in_gain, z_w, x_w, bc_w, dt_w, cx_w, cx_b, cbc_w, cbc_b, cx_s, cbc_s,
@@ -76,8 +75,8 @@
         out_layer, out_cx, out_cbc, out_state,
         zw, xw, bcw, dtw, cxs, cbcs, st, ow, gain, slot_v, slot_m, act_v, cxw, cxb, cbcw, cbcb, ngain,
         dtb_m, rate_m, skip_m,
-        stb, xn, hid_recv, bc_send, bc_recv, sq_send, sq_recv, br_send, br_recv,
-        in_sem, send_sem, recv_sem, relay_sem,
+        stb, xn, hid_recv, side, bc_send, bc_recv, br_send, br_recv,
+        in_sem, send_sem, recv_sem, relay_sem, side_sem,
     ):
         me = lax.axis_index("tp")
         chip, core = me // 2, lax.rem(me, 2)
@@ -106,7 +105,7 @@
         load("slot", slot, slot_v)
         load("slot_m", slot, slot_m)
         load("act", act, act_v)
-        load("bc_w", bc_w, bcw)
+        load("bc_w", bc_w, bcw.at[core])
         load("in_gain", in_gain, gain)
         load("cbc_s", cbc_s, cbcs)
         load("cbc_w", cbc_w, cbcw)
@@ -172,6 +171,23 @@
         bc_cols = dot_nt(mirror, bc_rows.astype(BF16))
         bc_old = [dot_nt(mirror, dot(to_seq, cbcs[k]).astype(BF16)) for k in range(3)]
         bc_base = (bc_old[0] * bc_cols[:, 0:1] + bc_old[1] * bc_cols[:, 1:2]) + bc_old[2] * bc_cols[:, 2:3]
+        pad = jnp.zeros((bc_dev, LANES - seqs), F32)
+        side[core, 0] = jnp.concatenate([bc_base + bc_cols[:, 4:5], pad], axis=1)
+        side[core, 1] = jnp.broadcast_to(bc_cols[:, 3:4], (bc_dev, LANES))
+        loads["bc_w"].wait()
+        bcw[core] = dot(mirror, bcw[core]).astype(BF16)
+
+        def lend(j, ref):
+            return pltpu.make_async_remote_copy(
+                src_ref=ref.at[0], dst_ref=ref.at[0], send_sem=side_sem.at[0, j], recv_sem=side_sem.at[1, j],
+                device_id=device(0, 1), device_id_type=MESH,
+            )
+
+        @pl.when(core == 0)
+        def _():
+            lend(0, side).start()
+            lend(1, bcw).start()
+
         for name in ("cx_s", "cx_w", "cx_b", "norm_gain", "dt_bias", "log_rate", "skip_gain"):
             loads[name].wait()
         eye_ch = eye(chans)
@@ -191,9 +207,7 @@
             return carry
 
         lax.fori_loop(0, seqs, narrow, 0)
-        for name in ("bc_w", "dt_w"):
-            loads[name].wait()
-        bcw[...] = dot(mirror, bcw[...]).astype(BF16)
+        loads["dt_w"].wait()
 
         pltpu.make_async_remote_copy(
             src_ref=hid_recv.at[pl.ds(1, n_tp - 1)], dst_ref=hid_recv.at[pl.ds(1, n_tp - 1)],
@@ -209,45 +223,47 @@
             hid_recv[2 * lax.rem(t // 2 - chip + chips, chips) + t % 2].astype(F32) for t in range(n_tp)
         ]
         whole = jnp.concatenate(blocks, axis=1)
+        for k in range(tiles):
+            at = slice(k * LANES, (k + 1) * LANES)
+            xn[:, at] = (whole[:, at] * gain[k : k + 1, :]).astype(BF16)
         squares = whole[:, :LANES] * whole[:, :LANES]
         for k in range(1, tiles):
             part = whole[:, k * LANES : (k + 1) * LANES]
             squares = squares + part * part
-        inv = lax.rsqrt(jnp.sum(squares, axis=1, keepdims=True) / width + EPS)
-        for k in range(tiles):
-            at = slice(k * LANES, (k + 1) * LANES)
-            xn[:, at] = (whole[:, at] * inv * gain[k : k + 1, :]).astype(BF16)
-
-        bc_proj = dot_nt(bcw[...], xn[...]).astype(BF16)
-        bc_conv = silu(bc_base + bc_proj.astype(F32) * bc_cols[:, 3:4] + bc_cols[:, 4:5]).astype(BF16).astype(F32)
-        spread = jnp.concatenate([bc_conv, jnp.zeros((bc_dev, LANES - seqs), F32)], axis=1)
-        spread = pltpu.roll(spread, 0, 1, stride=seqs, stride_axis=0)
-        bc_send[...] = jnp.sum(spread.reshape(bc_dev // SUBS, SUBS, LANES), axis=1)
-
-        def exchange(phase, src_of, dst_ref):
-            for step, flip in partners:
-                peer = lax.rem(chip + step, chips) * 2 + (lax.rem(core + 1, 2) if flip else core)
-                pltpu.make_async_remote_copy(
-                    src_ref=src_of(peer), dst_ref=dst_ref.at[me],
-                    send_sem=send_sem.at[phase], recv_sem=recv_sem.at[phase],
-                    device_id={"tp": peer}, device_id_type=MESH,
-                ).start()
-
-        def all_of(phase, dst_ref):
+        inv_col = lax.rsqrt(jnp.sum(squares, axis=1, keepdims=True) / width + EPS)
+        inv = jnp.sum(jnp.where(diagonal, jnp.broadcast_to(inv_col, (seqs, seqs)), 0.0), axis=0, keepdims=True)
+
+        def all_of(phase, dst_ref, count):
             return pltpu.make_async_remote_copy(
-                src_ref=dst_ref.at[pl.ds(0, others)], dst_ref=dst_ref.at[pl.ds(0, others)],
+                src_ref=dst_ref.at[pl.ds(0, count)], dst_ref=dst_ref.at[pl.ds(0, count)],
                 send_sem=send_sem.at[phase], recv_sem=recv_sem.at[phase],
                 device_id=device(0, 1 - core), device_id_type=MESH,
             )
 
-        exchange(1, lambda peer: bc_send, bc_recv)
-        bc_recv[me] = bc_send[...]
-
-        dt_proj = dot_nt(dtw[...], xn[...]).astype(BF16).astype(F32)
+        @pl.when(core == 1)
+        def _():
+            for j, ref in ((0, side), (1, bcw)):
+                lend(j, ref).wait_recv()
+            both = 2 * bc_dev
+            base = jnp.concatenate([side[0, 0], side[1, 0]], axis=0)[:, :seqs]
+            tap = jnp.concatenate([side[0, 1], side[1, 1]], axis=0)[:, :seqs]
+            proj = dot_nt(jnp.concatenate([bcw[0], bcw[1]], axis=0), xn[...])
+            bc_conv = silu(base + (proj * inv).astype(BF16).astype(F32) * tap).astype(BF16).astype(F32)
+            spread = jnp.concatenate([bc_conv, jnp.zeros((both, LANES - seqs), F32)], axis=1)
+            spread = pltpu.roll(spread.reshape(both // SUBS, SUBS, LANES), 0, 2, stride=seqs, stride_axis=1)
+            bc_send[...] = jnp.sum(spread, axis=1)
+            for step, which in [(step, which) for step in steps_far for which in (0, 1)] + [(0, 0)]:
+                pltpu.make_async_remote_copy(
+                    src_ref=bc_send, dst_ref=bc_recv.at[chip], send_sem=send_sem.at[1], recv_sem=recv_sem.at[1],
+                    device_id=device(step, which), device_id_type=MESH,
+                ).start()
+            bc_recv[chip] = bc_send[...]
+
+        dt_proj = (dot_nt(dtw[...], xn[...]) * inv).astype(BF16).astype(F32)
         loads["x_w"].wait()
-        x_proj = dot_nt(xw[...], xn[...]).astype(BF16)
+        x_proj = (dot_nt(xw[...], xn[...]) * inv).astype(BF16)
         loads["z_w"].wait()
-        z_proj = dot_nt(zw[...], xn[...]).astype(BF16)
+        z_proj = (dot_nt(zw[...], xn[...]) * inv).astype(BF16)
         x_conv = silu(x_base + x_proj.astype(F32) * cols[:, 3:4] + cols[:, 4:5]).astype(BF16)
         x_f = x_conv.astype(F32)
         z_gate = silu(z_proj.astype(F32))
@@ -266,13 +282,21 @@
         decay = per_channel(decays)
         skipped = jnp.concatenate([jnp.full((HP, seqs), skip_m[h], F32) for h in range(heads)], axis=0) * x_f
 
-        all_of(1, bc_recv).wait_recv()
+        @pl.when(core == 0)
+        def _():
+            all_of(1, bc_recv, chips).wait_recv()
+
+        @pl.when(core == 1)
+        def _():
+            all_of(1, bc_recv, chips - 1).wait_recv()
+
 
         def unpacked(at):
             found = []
             for row in range(NS // SUBS):
                 line = at // SUBS + row
-                packed = bc_recv[line // (bc_dev // SUBS), pl.ds(line % (bc_dev // SUBS), 1), :]
+                lines = 2 * bc_dev // SUBS
+                packed = bc_recv[line // lines, pl.ds(line % lines, 1), :]
                 found.append(
                     pltpu.roll(jnp.broadcast_to(packed, (SUBS, LANES)), 0, 1, stride=seqs, stride_axis=0)
                 )
@@ -287,23 +311,44 @@
         y = (decay * s_c + dtx * bc_dot) + skipped
         gated = y * z_gate
         scaled = (gated * gain_col).astype(BF16)
-        sq_send[...] = jnp.concatenate(
-            [jnp.sum(gated * gated, axis=0, keepdims=True), jnp.zeros((1, LANES - seqs), F32)], axis=1
-        )
-        exchange(2, lambda peer: sq_send, sq_recv)
+        sq_row = jnp.broadcast_to(jnp.sum(gated * gated, axis=0, keepdims=True), (seqs, seqs))
+        sq_col = jnp.sum(jnp.where(diagonal, sq_row, 0.0), axis=1, keepdims=True)
+        sq_1 = sq_col.astype(BF16).astype(F32)
+        sq_2 = (sq_col - sq_1).astype(BF16).astype(F32)
+        sq_terms = (sq_1, sq_2, (sq_col - sq_1) - sq_2)
         loads["out_w"].wait()
-        branch = dot(dot_nt(eye16, scaled).astype(BF16), ow[...])
-        for k in range(tiles):
-            br_send[k] = branch[:, k * LANES : (k + 1) * LANES].astype(BF16)
-
-        def first_tile(who):
-            return (who * feats) // LANES
-
-        exchange(3, lambda peer: br_send.at[pl.ds(first_tile(peer), 2)], br_recv)
-        br_recv[me] = br_send[pl.ds(first_tile(me), 2)]
-        sq_recv[me] = sq_send[...]
+        rows_seq = dot_nt(eye16, scaled).astype(BF16)
+        lane_at = iota((seqs, LANES), 1)
+        side_of = chip // half
+        half_width = half * 2 * feats
+        for part in range(2):
+            which = 1 - side_of if part == 0 else side_of
+            columns = ow[:, pl.ds(pl.multiple_of(which * half_width, LANES), half_width)]
+            branch = dot(rows_seq, columns)
+            for i in range(2 * half):
+                first, start = (i * feats) // LANES, (i * feats) % LANES
+                free = (start + feats) % (2 * LANES)
+                for k in range(2):
+                    tile = branch[:, (first + k) * LANES : (first + k + 1) * LANES]
+                    if free // LANES == k:
+                        for j, term in enumerate(sq_terms):
+                            tile = jnp.where(lane_at == free % LANES + j, term, tile)
+                    br_send[which * 2 * half + i, k] = tile.astype(BF16)
+            for i in range(half):
+                far = which * half + lax.rem(chip + i, half)
+                for flip in (1, 0):
+                    if part == 1 and i == 0 and not flip:
+                        continue
+                    peer = far * 2 + (1 - core if flip else core)
+                    pltpu.make_async_remote_copy(
+                        src_ref=br_send.at[peer], dst_ref=br_recv.at[me],
+                        send_sem=send_sem.at[2], recv_sem=recv_sem.at[2],
+                        device_id={"tp": peer}, device_id_type=MESH,
+                    ).start()
+        br_recv[me] = br_send[me]
 
         x_now = dot_nt(to_slot, x_proj)
+        bc_proj = (dot_nt(bcw[core], xn[...]) * inv).astype(BF16)
         bc_now = dot(dot_nt(to_slot, bc_proj).astype(BF16), mirror)
         for out, old, now in ((out_cx, cxs, x_now), (out_cbc, cbcs, bc_now)):
             held = [old[k].astype(F32) for k in range(3)]
@@ -320,25 +365,20 @@
             grown = dtx_slot[:, b : b + 1] * b_rows[b : b + 1, :]
             out_state[b] = decay_slot[:, b : b + 1] * st[b] + grown
 
-        all_of(2, sq_recv).wait_recv()
-        total_sq = sq_recv[0]
-        for t in range(1, n_tp):
-            total_sq = total_sq + sq_recv[t]
-        sq_all = jnp.broadcast_to(total_sq[:, :seqs], (seqs, seqs))
-        sq_col = jnp.sum(jnp.where(diagonal, sq_all, 0.0), axis=1, keepdims=True)
-        inv_out = lax.rsqrt(sq_col / INNER + EPS)
-        all_of(3, br_recv).wait_recv()
+        all_of(2, br_recv, others).wait_recv()
         sums = [br_recv[0, k].astype(F32) for k in range(2)]
         for t in range(1, n_tp):
             sums = [sums[k] + br_recv[t, k].astype(F32) for k in range(2)]
         shift = lax.rem(me * feats, LANES)
-        branch_sum = pltpu.roll(jnp.concatenate(sums, axis=1), lax.rem(2 * LANES - shift, 2 * LANES), 1)[:, :feats]
+        summed = pltpu.roll(jnp.concatenate(sums, axis=1), lax.rem(2 * LANES - shift, 2 * LANES), 1)
+        branch_sum = summed[:, :feats]
+        sq_total = (summed[:, feats : feats + 1] + summed[:, feats + 1 : feats + 2]) + summed[:, feats + 2 : feats + 3]
+        inv_out = lax.rsqrt(sq_total / INNER + EPS)
         kept = hid_recv[core].astype(F32)
         fresh = (kept + inv_out * branch_sum).astype(BF16).astype(F32)
         out_layer[...] = jnp.where(act_col, fresh, kept).astype(BF16)
 
-        for phase, ref in ((1, bc_recv), (2, sq_recv), (3, br_recv)):
-            all_of(phase, ref).wait_send()
+        all_of(2, br_recv, others).wait_send()
 
         def hid_sent(count):
             return pltpu.make_async_remote_copy(
@@ -350,11 +390,14 @@
         @pl.when(core == 0)
         def _():
             hid_sent(chips).wait_send()
+            for j, ref in ((0, side), (1, bcw)):
+                lend(j, ref).wait_send()
 
         @pl.when(core == 1)
         def _():
             hid_sent(chips - 1).wait_send()
             relay().wait_send()
+            all_of(1, bc_recv, others).wait_send()
 
     return body
 
@@ -388,7 +431,7 @@
         scratch_shapes=[
             pltpu.VMEM((chans, width), BF16),
             pltpu.VMEM((chans, width), BF16),
-            pltpu.VMEM((bc_dev, width), BF16),
+            pltpu.VMEM((2, bc_dev, width), BF16),
             pltpu.VMEM((heads, width), BF16),
             pltpu.VMEM((3, seqs, chans), BF16),
             pltpu.VMEM((3, seqs, bc_dev), BF16),
@@ -409,16 +452,16 @@
             pltpu.VMEM((seqs, chans, NS), BF16),
             pltpu.VMEM((seqs, width), BF16),
             pltpu.VMEM((n_tp, seqs, feats), BF16),
-            pltpu.VMEM((bc_dev // SUBS, LANES), F32),
-            pltpu.VMEM((n_tp, bc_dev // SUBS, LANES), F32),
-            pltpu.VMEM((1, LANES), F32),
-            pltpu.VMEM((n_tp, 1, LANES), F32),
-            pltpu.VMEM((tiles, seqs, LANES), BF16),
+            pltpu.VMEM((2, 2, bc_dev, LANES), F32),
+            pltpu.VMEM((2 * bc_dev // SUBS, LANES), F32),
+            pltpu.VMEM((n_tp, 2 * bc_dev // SUBS, LANES), F32),
             pltpu.VMEM((n_tp, 2, seqs, LANES), BF16),
-            pltpu.SemaphoreType.DMA((21,)),
-            pltpu.SemaphoreType.DMA((4,)),
-            pltpu.SemaphoreType.DMA((4,)),
+            pltpu.VMEM((n_tp, 2, seqs, LANES), BF16),
+            pltpu.SemaphoreType.DMA((20 + 1,)),
+            pltpu.SemaphoreType.DMA((3,)),
+            pltpu.SemaphoreType.DMA((3,)),
             pltpu.SemaphoreType.DMA((1,)),
+            pltpu.SemaphoreType.DMA((2, 2)),
         ],
         compiler_params=pltpu.CompilerParams(
             collective_id=0, has_side_effects=True, vmem_limit_bytes=60 * 1024 * 1024

time: 39.9 us -> 38 us (0.952)
  Pallas kernels: 39.1 us -> 37.3 us
    pallas_call x1, Pallas kernels: 37.6 us -> 35.7 us  [shards(): pl.pallas_call(make_kernel(n_tp, seqs, feats, heads, chans, bc_dev), out_...]
where the time goes in v4:
time: 38 us; the launch traced here: 37.9 us
  Pallas kernels  37.3 us (98%)
  between operations  0.65 us (2%)
    pallas_call x1, Pallas kernels, shards(): pl.pallas_call(make_kernel(n_tp, seqs, feats, heads, chans, bc_dev), out_...  35.7 us
    pallas_call x1, Pallas kernels, shards(): pl.pallas_call(put_out, out_shape=tuple((shape(dims, kind) for dims, kind...  1.53 us

profile of v4, /device:TPU:513, one launch (start us, length us, event | category | flops | bytes accessed | tf_op | source)
XLA Modules:
  0.0 37.9 jit_solution(15381472138891261961)
XLA Ops:
  0.6 35.7 %step.1 = (bf16[16,160]{1,0:T(8,128)(2,1)S(1)}, bf16[3,16,320]{2,1,0:T(8,128)(2,1)S(1)}, bf16[3,16,16]{2,1,0:T(8,128)(2,1)S(1)}, f32[16,320,128]{2,1,0:T(8,128)S(1)}) custom-call(bf16[16,160]{1,0:T(8,128)(2,1)} %hid.1, s32[1,16]{1,0:T(1,128)} %slot.1, s32[1,16]{1,0:T(1,128)} %bitcast.21, f32[20,128]{1,0:T(8,128)} %bitcast.19, bf16[320,2560]{1,0:T(8,128)(2,1)} %bitcast.14, ...), custom_call_target="tpu_custom_call" | custom-call | tf_op jit(solution)/shard_map/step/pallas_call | solution.py:426
  36.4 1.5 %put.1 = (bf16[16,160]{1,0:T(8,128)(2,1)}, bf16[3,16,320]{2,1,0:T(8,128)(2,1)}, bf16[3,16,16]{2,1,0:T(8,128)(2,1)}, f32[16,320,128]{2,1,0:T(8,128)}) custom-call(bf16[16,160]{1,0:T(8,128)(2,1)S(1)} %get-tuple-element.12.refs_0_, bf16[3,16,320]{2,1,0:T(8,128)(2,1)S(1)} %get-tuple-element.13.refs_1_, bf16[3,16,16]{2,1,0:T(8,128)(2,1)S(1)} %get-tuple-element.14.refs_2_, ...), custom_call_target="tpu_custom_call" | custom-call | tf_op jit(solution)/shard_map/put/pallas_call | solution.py:478

commit v5 on v4

--- a/solution.py
+++ b/solution.py
@@ -52,7 +52,13 @@
 
 def put_out(*refs):
     sems = refs[-1]
-    copies = [pltpu.make_async_copy(refs[k], refs[4 + k], sems.at[k]) for k in (3, 0, 1, 2)]
+    pieces = 4
+    rows = refs[3].shape[0] // pieces
+    copies = [
+        pltpu.make_async_copy(refs[3].at[pl.ds(k * rows, rows)], refs[7].at[pl.ds(k * rows, rows)], sems.at[3 + k])
+        for k in range(pieces)
+    ]
+    copies += [pltpu.make_async_copy(refs[k], refs[4 + k], sems.at[k]) for k in range(3)]
     for copy in copies:
         copy.start()
     for copy in copies:
@@ -247,7 +253,8 @@
             both = 2 * bc_dev
             base = jnp.concatenate([side[0, 0], side[1, 0]], axis=0)[:, :seqs]
             tap = jnp.concatenate([side[0, 1], side[1, 1]], axis=0)[:, :seqs]
-            proj = dot_nt(jnp.concatenate([bcw[0], bcw[1]], axis=0), xn[...])
+            weights = jnp.concatenate([bcw[0], bcw[1]], axis=0)
+            proj = dot_nt(weights[:, : width // 2], xn[:, : width // 2]) + dot_nt(weights[:, width // 2 :], xn[:, width // 2 :])
             bc_conv = silu(base + (proj * inv).astype(BF16).astype(F32) * tap).astype(BF16).astype(F32)
             spread = jnp.concatenate([bc_conv, jnp.zeros((both, LANES - seqs), F32)], axis=1)
             spread = pltpu.roll(spread.reshape(both // SUBS, SUBS, LANES), 0, 2, stride=seqs, stride_axis=1)
@@ -261,8 +268,8 @@
 
         dt_proj = (dot_nt(dtw[...], xn[...]) * inv).astype(BF16).astype(F32)
         loads["x_w"].wait()
+        loads["z_w"].wait()
         x_proj = (dot_nt(xw[...], xn[...]) * inv).astype(BF16)
-        loads["z_w"].wait()
         z_proj = (dot_nt(zw[...], xn[...]) * inv).astype(BF16)
         x_conv = silu(x_base + x_proj.astype(F32) * cols[:, 3:4] + cols[:, 4:5]).astype(BF16)
         x_f = x_conv.astype(F32)
@@ -305,8 +312,11 @@
         c_f, b_f = unpacked(NS), unpacked(0)
         lane = iota((NS, seqs), 1)
         c_big = jnp.concatenate([jnp.where(lane == b, c_f, 0.0).astype(BF16) for b in range(seqs)], axis=0)
-        s_big = jnp.concatenate([stb[b] for b in range(seqs)], axis=1)
-        s_c = dot(s_big, c_big)
+        s_c = []
+        for at in (0, chans // 2):
+            s_big = jnp.concatenate([stb[b, at : at + chans // 2, :] for b in range(seqs)], axis=1)
+            s_c.append(dot(s_big, c_big))
+        s_c = jnp.concatenate(s_c, axis=0)
         bc_dot = jnp.sum(b_f * c_f, axis=0, keepdims=True)
         y = (decay * s_c + dtx * bc_dot) + skipped
         gated = y * z_gate
@@ -323,8 +333,14 @@
         half_width = half * 2 * feats
         for part in range(2):
             which = 1 - side_of if part == 0 else side_of
-            columns = ow[:, pl.ds(pl.multiple_of(which * half_width, LANES), half_width)]
-            branch = dot(rows_seq, columns)
+            step = 2 * LANES
+            branch = jnp.concatenate(
+                [
+                    dot(rows_seq, ow[:, pl.ds(pl.multiple_of(which * half_width + at, LANES), step)])
+                    for at in range(0, half_width, step)
+                ],
+                axis=1,
+            )
             for i in range(2 * half):
                 first, start = (i * feats) // LANES, (i * feats) % LANES
                 free = (start + feats) % (2 * LANES)
@@ -480,7 +496,7 @@
         out_shape=tuple(shape(dims, kind) for dims, kind in results),
         in_specs=[vmem] * 4,
         out_specs=(hbm,) * 4,
-        scratch_shapes=[pltpu.SemaphoreType.DMA((4,))],
+        scratch_shapes=[pltpu.SemaphoreType.DMA((7,))],
         name="put",
     )(*(pltpu.with_memory_space_constraint(x, pltpu.VMEM) for x in made))
     return (

time: 38 us -> 37.8 us (level)
  no operation moved by 1% of the time
where the time goes in v5:
time: 37.8 us; the launch traced here: 37.7 us
  Pallas kernels  37 us (98%)
  between operations  0.65 us (2%)
    pallas_call x1, Pallas kernels, shards(): pl.pallas_call(make_kernel(n_tp, seqs, feats, heads, chans, bc_dev), out_...  35.5 us
    pallas_call x1, Pallas kernels, shards(): pl.pallas_call(put_out, out_shape=tuple((shape(dims, kind) for dims, kind...  1.55 us

profile of v5, /device:TPU:513, one launch (start us, length us, event | category | flops | bytes accessed | tf_op | source)
XLA Modules:
  0.0 37.7 jit_solution(7823930402830017632)
XLA Ops:
  0.6 35.5 %step.1 = (bf16[16,160]{1,0:T(8,128)(2,1)S(1)}, bf16[3,16,320]{2,1,0:T(8,128)(2,1)S(1)}, bf16[3,16,16]{2,1,0:T(8,128)(2,1)S(1)}, f32[16,320,128]{2,1,0:T(8,128)S(1)}) custom-call(bf16[16,160]{1,0:T(8,128)(2,1)} %hid.1, s32[1,16]{1,0:T(1,128)} %slot.1, s32[1,16]{1,0:T(1,128)} %bitcast.21, f32[20,128]{1,0:T(8,128)} %bitcast.19, bf16[320,2560]{1,0:T(8,128)(2,1)} %bitcast.14, ...), custom_call_target="tpu_custom_call" | custom-call | tf_op jit(solution)/shard_map/step/pallas_call | solution.py:442
  36.1 1.6 %put.1 = (bf16[16,160]{1,0:T(8,128)(2,1)}, bf16[3,16,320]{2,1,0:T(8,128)(2,1)}, bf16[3,16,16]{2,1,0:T(8,128)(2,1)}, f32[16,320,128]{2,1,0:T(8,128)}) custom-call(bf16[16,160]{1,0:T(8,128)(2,1)S(1)} %get-tuple-element.12.refs_0_, bf16[3,16,320]{2,1,0:T(8,128)(2,1)S(1)} %get-tuple-element.13.refs_1_, bf16[3,16,16]{2,1,0:T(8,128)(2,1)S(1)} %get-tuple-element.14.refs_2_, ...), custom_call_target="tpu_custom_call" | custom-call | tf_op jit(solution)/shard_map/put/pallas_call | solution.py:494

commit v6 on v5

--- a/solution.py
+++ b/solution.py
@@ -325,10 +325,22 @@
         sq_col = jnp.sum(jnp.where(diagonal, sq_row, 0.0), axis=1, keepdims=True)
         sq_1 = sq_col.astype(BF16).astype(F32)
         sq_2 = (sq_col - sq_1).astype(BF16).astype(F32)
-        sq_terms = (sq_1, sq_2, (sq_col - sq_1) - sq_2)
+        sq_cols = [half_rows for term in (sq_1, sq_2, (sq_col - sq_1) - sq_2) for half_rows in (term[:SUBS], term[SUBS:])]
         loads["out_w"].wait()
         rows_seq = dot_nt(eye16, scaled).astype(BF16)
-        lane_at = iota((seqs, LANES), 1)
+        lane_at = iota((SUBS, LANES), 1)
+        spare = feats - LANES
+        tails = {}
+        for start in sorted({(t * feats) % LANES for t in range(n_tp)}):
+            tail = jnp.zeros((SUBS, LANES), F32)
+            for j, term in enumerate(sq_cols):
+                tail = jnp.where(lane_at == (start + 2 * spare + j) % LANES, term, tail)
+            tails[start] = tail
+
+        def within(at):
+            at = at % LANES
+            return (lane_at >= at) & (lane_at < at + spare)
+
         side_of = chip // half
         half_width = half * 2 * feats
         for part in range(2):
@@ -343,13 +355,12 @@
             )
             for i in range(2 * half):
                 first, start = (i * feats) // LANES, (i * feats) % LANES
-                free = (start + feats) % (2 * LANES)
-                for k in range(2):
-                    tile = branch[:, (first + k) * LANES : (first + k + 1) * LANES]
-                    if free // LANES == k:
-                        for j, term in enumerate(sq_terms):
-                            tile = jnp.where(lane_at == free % LANES + j, term, tile)
-                    br_send[which * 2 * half + i, k] = tile.astype(BF16)
+                tile_0 = branch[:, first * LANES : (first + 1) * LANES]
+                tile_1 = branch[:, (first + 1) * LANES : (first + 2) * LANES]
+                main = jnp.where(iota((seqs, LANES), 1) >= start, tile_0, tile_1)
+                rest = jnp.where(within(start + spare), pltpu.roll(tile_1[SUBS:], spare, 1), tails[start])
+                rest = jnp.where(within(start), tile_1[:SUBS], rest)
+                br_send[which * 2 * half + i] = jnp.concatenate([main, rest], axis=0).astype(BF16)
             for i in range(half):
                 far = which * half + lax.rem(chip + i, half)
                 for flip in (1, 0):
@@ -382,14 +393,20 @@
             out_state[b] = decay_slot[:, b : b + 1] * st[b] + grown
 
         all_of(2, br_recv, others).wait_recv()
-        sums = [br_recv[0, k].astype(F32) for k in range(2)]
+        total = br_recv[0].astype(F32)
         for t in range(1, n_tp):
-            sums = [sums[k] + br_recv[t, k].astype(F32) for k in range(2)]
+            total = total + br_recv[t].astype(F32)
         shift = lax.rem(me * feats, LANES)
-        summed = pltpu.roll(jnp.concatenate(sums, axis=1), lax.rem(2 * LANES - shift, 2 * LANES), 1)
-        branch_sum = summed[:, :feats]
-        sq_total = (summed[:, feats : feats + 1] + summed[:, feats + 1 : feats + 2]) + summed[:, feats + 2 : feats + 3]
-        inv_out = lax.rsqrt(sq_total / INNER + EPS)
+        total = pltpu.roll(total, lax.rem(LANES - shift, LANES), 1)
+        rest = total[seqs:]
+        rest = jnp.concatenate([rest, pltpu.roll(rest, LANES - spare, 1)], axis=0)
+        branch_sum = jnp.concatenate([total[:seqs], rest[:, :spare]], axis=1)
+        sq_at = 2 * spare
+        sq_rows = [
+            (total[seqs:, at : at + 1] + total[seqs:, at + 2 : at + 3]) + total[seqs:, at + 4 : at + 5]
+            for at in (sq_at, sq_at + 1)
+        ]
+        inv_out = lax.rsqrt(jnp.concatenate(sq_rows, axis=0) / INNER + EPS)
         kept = hid_recv[core].astype(F32)
         fresh = (kept + inv_out * branch_sum).astype(BF16).astype(F32)
         out_layer[...] = jnp.where(act_col, fresh, kept).astype(BF16)
@@ -471,8 +488,8 @@
             pltpu.VMEM((2, 2, bc_dev, LANES), F32),
             pltpu.VMEM((2 * bc_dev // SUBS, LANES), F32),
             pltpu.VMEM((n_tp, 2 * bc_dev // SUBS, LANES), F32),
-            pltpu.VMEM((n_tp, 2, seqs, LANES), BF16),
-            pltpu.VMEM((n_tp, 2, seqs, LANES), BF16),
+            pltpu.VMEM((n_tp, seqs + SUBS, LANES), BF16),
+            pltpu.VMEM((n_tp, seqs + SUBS, LANES), BF16),
             pltpu.SemaphoreType.DMA((20 + 1,)),
             pltpu.SemaphoreType.DMA((3,)),
             pltpu.SemaphoreType.DMA((3,)),

time: 37.8 us -> 37.2 us (0.984)
  Pallas kernels: 37 us -> 36.4 us
    pallas_call x1, Pallas kernels: 35.5 us -> 34.8 us  [shards(): pl.pallas_call(make_kernel(n_tp, seqs, feats, heads, chans, bc_dev), out_...]
where the time goes in v6:
time: 37.2 us; the launch traced here: 37 us
  Pallas kernels  36.4 us (98%)
  between operations  0.65 us (2%)
    pallas_call x1, Pallas kernels, shards(): pl.pallas_call(make_kernel(n_tp, seqs, feats, heads, chans, bc_dev), out_...  34.8 us
    pallas_call x1, Pallas kernels, shards(): pl.pallas_call(put_out, out_shape=tuple((shape(dims, kind) for dims, kind...  1.55 us

profile of v6, /device:TPU:513, one launch (start us, length us, event | category | flops | bytes accessed | tf_op | source)
XLA Modules:
  0.0 37.0 jit_solution(18432699433583290176)
XLA Ops:
  0.6 34.8 %step.1 = (bf16[16,160]{1,0:T(8,128)(2,1)S(1)}, bf16[3,16,320]{2,1,0:T(8,128)(2,1)S(1)}, bf16[3,16,16]{2,1,0:T(8,128)(2,1)S(1)}, f32[16,320,128]{2,1,0:T(8,128)S(1)}) custom-call(bf16[16,160]{1,0:T(8,128)(2,1)} %hid.1, s32[1,16]{1,0:T(1,128)} %slot.1, s32[1,16]{1,0:T(1,128)} %bitcast.21, f32[20,128]{1,0:T(8,128)} %bitcast.19, bf16[320,2560]{1,0:T(8,128)(2,1)} %bitcast.14, ...), custom_call_target="tpu_custom_call" | custom-call | tf_op jit(solution)/shard_map/step/pallas_call | solution.py:459
  35.5 1.6 %put.1 = (bf16[16,160]{1,0:T(8,128)(2,1)}, bf16[3,16,320]{2,1,0:T(8,128)(2,1)}, bf16[3,16,16]{2,1,0:T(8,128)(2,1)}, f32[16,320,128]{2,1,0:T(8,128)}) custom-call(bf16[16,160]{1,0:T(8,128)(2,1)S(1)} %get-tuple-element.12.refs_0_, bf16[3,16,320]{2,1,0:T(8,128)(2,1)S(1)} %get-tuple-element.13.refs_1_, bf16[3,16,16]{2,1,0:T(8,128)(2,1)S(1)} %get-tuple-element.14.refs_2_, ...), custom_call_target="tpu_custom_call" | custom-call | tf_op jit(solution)/shard_map/put/pallas_call | solution.py:511

commit v7 on v6

--- a/solution.py
+++ b/solution.py
@@ -81,11 +81,13 @@
         out_layer, out_cx, out_cbc, out_state,
         zw, xw, bcw, dtw, cxs, cbcs, st, ow, gain, slot_v, slot_m, act_v, cxw, cxb, cbcw, cbcb, ngain,
         dtb_m, rate_m, skip_m,
-        stb, xn, hid_recv, side, bc_send, bc_recv, br_send, br_recv,
+        stb, xn, hid_recv, side, bcw_send, bcw_recv, bc_sums, br_send, br_recv,
         in_sem, send_sem, recv_sem, relay_sem, side_sem,
     ):
         me = lax.axis_index("tp")
         chip, core = me // 2, lax.rem(me, 2)
+        row = lax.axis_index("dp")
+        odd = lax.rem(row, 2)
         barrier = pltpu.get_barrier_semaphore()
 
         def device(step, which):
@@ -108,10 +110,20 @@
             for step in steps_far:
                 pl.semaphore_signal(barrier, inc=1, device_id=device(step, 1), device_id_type=MESH)
 
+            @pl.when(odd == 0)
+            def _():
+                for t in range(n_tp):
+                    pl.semaphore_signal(barrier, inc=1, device_id={"tp": t, "dp": row + 1}, device_id_type=MESH)
+
+            @pl.when(odd == 1)
+            def _():
+                for step in steps_far:
+                    pl.semaphore_signal(barrier, inc=1, device_id=device(step, 0), device_id_type=MESH)
+
         load("slot", slot, slot_v)
         load("slot_m", slot, slot_m)
         load("act", act, act_v)
-        load("bc_w", bc_w, bcw.at[core])
+        load("bc_w", bc_w, bcw)
         load("in_gain", in_gain, gain)
         load("cbc_s", cbc_s, cbcs)
         load("cbc_w", cbc_w, cbcw)
@@ -129,10 +141,10 @@
         load("z_w", z_w, zw)
         load("out_w", out_w, ow)
 
-        def first_send(step, which, dst_slot):
+        def first_send(step, which, dst_slot, phase=0):
             return pltpu.make_async_remote_copy(
                 src_ref=hid_recv.at[core], dst_ref=hid_recv.at[dst_slot],
-                send_sem=send_sem.at[0], recv_sem=recv_sem.at[0],
+                send_sem=send_sem.at[phase], recv_sem=recv_sem.at[phase],
                 device_id=device(step, which), device_id_type=MESH,
             )
 
@@ -146,15 +158,15 @@
         @pl.when(core == 0)
         def _():
             loads["hid"].wait()
-            pl.semaphore_wait(barrier, 1)
+            pl.semaphore_wait(barrier, 1 + odd * (2 * chips - 1))
+            first_send(0, 1, 0, 4).start()
             for step in steps_far:
                 first_send(step, 1, 2 * (chips - step)).start()
-            first_send(0, 1, 0).start()
 
         @pl.when(core == 1)
         def _():
             loads["hid"].wait()
-            pl.semaphore_wait(barrier, chips)
+            pl.semaphore_wait(barrier, chips + odd * chips)
             pl.semaphore_signal(barrier, inc=1, device_id=device(0, 0), device_id_type=MESH)
             for step in steps_far:
                 first_send(step, 1, 2 * (chips - step) + 1).start()
@@ -180,19 +192,46 @@
         pad = jnp.zeros((bc_dev, LANES - seqs), F32)
         side[core, 0] = jnp.concatenate([bc_base + bc_cols[:, 4:5], pad], axis=1)
         side[core, 1] = jnp.broadcast_to(bc_cols[:, 3:4], (bc_dev, LANES))
+        def lend():
+            return pltpu.make_async_remote_copy(
+                src_ref=side.at[0], dst_ref=side.at[0], send_sem=side_sem.at[0], recv_sem=side_sem.at[1],
+                device_id=device(0, 1), device_id_type=MESH,
+            )
+
+        @pl.when(core == 0)
+        def _():
+            lend().start()
+
         loads["bc_w"].wait()
-        bcw[core] = dot(mirror, bcw[core]).astype(BF16)
-
-        def lend(j, ref):
+        turned = dot(mirror, bcw[...]).astype(BF16)
+        bcw[...] = turned
+        for k in range(tiles):
+            bcw_send[k] = turned[:, k * LANES : (k + 1) * LANES]
+
+        def share_tile(of_chip):
+            return (of_chip * 2 * feats) // LANES
+
+        def share(of_chip, to_row):
             return pltpu.make_async_remote_copy(
-                src_ref=ref.at[0], dst_ref=ref.at[0], send_sem=side_sem.at[0, j], recv_sem=side_sem.at[1, j],
-                device_id=device(0, 1), device_id_type=MESH,
-            )
-
-        @pl.when(core == 0)
-        def _():
-            lend(0, side).start()
-            lend(1, bcw).start()
+                src_ref=bcw_send.at[pl.ds(share_tile(of_chip), 3)], dst_ref=bcw_recv.at[me],
+                send_sem=send_sem.at[3], recv_sem=recv_sem.at[3],
+                device_id={"tp": 2 * of_chip + 1, "dp": to_row}, device_id_type=MESH,
+            )
+
+        @pl.when(odd == 1)
+        def _():
+            for step in steps_far:
+                for to_row in (row - 1, row):
+                    share(lax.rem(chip + step, chips), to_row).start()
+            share(chip, row - 1).start()
+
+            @pl.when(core == 0)
+            def _():
+                share(chip, row).start()
+
+            @pl.when(core == 1)
+            def _():
+                bcw_recv[me] = bcw_send[pl.ds(share_tile(chip), 3)]
 
         for name in ("cx_s", "cx_w", "cx_b", "norm_gain", "dt_bias", "log_rate", "skip_gain"):
             loads[name].wait()
@@ -215,14 +254,65 @@
         lax.fori_loop(0, seqs, narrow, 0)
         loads["dt_w"].wait()
 
-        pltpu.make_async_remote_copy(
-            src_ref=hid_recv.at[pl.ds(1, n_tp - 1)], dst_ref=hid_recv.at[pl.ds(1, n_tp - 1)],
-            send_sem=send_sem.at[0], recv_sem=recv_sem.at[0],
-            device_id=device(0, 1 - core), device_id_type=MESH,
-        ).wait_recv()
+        def all_of(phase, dst_ref, count):
+            return pltpu.make_async_remote_copy(
+                src_ref=dst_ref.at[pl.ds(0, count)], dst_ref=dst_ref.at[pl.ds(0, count)],
+                send_sem=send_sem.at[phase], recv_sem=recv_sem.at[phase],
+                device_id=device(0, 1 - core), device_id_type=MESH,
+            )
+
+        lines = n_tp * bc_dev // SUBS
+        own_lines = 2 * bc_dev // SUBS
+
+        def packed(x):
+            count = x.shape[0]
+            spread = jnp.concatenate([x, jnp.zeros((count, LANES - seqs), F32)], axis=1)
+            spread = pltpu.roll(spread.reshape(count // SUBS, SUBS, LANES), 0, 2, stride=seqs, stride_axis=1)
+            return jnp.sum(spread, axis=1)
+
+        def relay_sums():
+            return pltpu.make_async_remote_copy(
+                src_ref=bc_sums, dst_ref=bc_sums, send_sem=relay_sem.at[1], recv_sem=recv_sem.at[1],
+                device_id=device(0, 0), device_id_type=MESH,
+            )
 
         @pl.when(core == 1)
         def _():
+            @pl.when(odd == 0)
+            def _():
+                all_of(3, bcw_recv, n_tp).wait_recv()
+
+            @pl.when(odd == 1)
+            def _():
+                all_of(3, bcw_recv, n_tp - 1).wait_recv()
+
+            first = share_tile(chip)
+            first_send(0, 1, 0, 4).wait_recv()
+            pair = jnp.concatenate([hid_recv[0].astype(F32), hid_recv[1].astype(F32), jnp.zeros((seqs, 3 * LANES - 2 * feats), F32)], axis=1)
+            pair = pltpu.roll(pair, lax.rem(chip * 2 * feats, LANES), 1)
+            terms = 0.0
+            for k in range(3):
+                scaled_k = (pair[:, k * LANES : (k + 1) * LANES] * gain[pl.ds(first + k, 1), :]).astype(BF16)
+                weights = jnp.concatenate([bcw_recv[t, k] for t in range(n_tp)], axis=0)
+                terms = terms + dot_nt(weights, scaled_k)
+            bc_sums[chip, 0:lines, :] = packed(terms)
+            lend().wait_recv()
+            for j in range(2):
+                own = packed(jnp.concatenate([side[0, j], side[1, j]], axis=0)[:, :seqs])
+                bc_sums[chip, lines + j * own_lines : lines + (j + 1) * own_lines, :] = own
+            for step in steps_far:
+                pltpu.make_async_remote_copy(
+                    src_ref=bc_sums.at[chip], dst_ref=bc_sums.at[chip], send_sem=send_sem.at[1], recv_sem=recv_sem.at[1],
+                    device_id=device(step, 1), device_id_type=MESH,
+                ).start()
+
+        @pl.when(core == 0)
+        def _():
+            all_of(0, hid_recv, n_tp - 1).wait_recv()
+
+        @pl.when(core == 1)
+        def _():
+            all_of(0, hid_recv, n_tp - 2).wait_recv()
             relay().start()
 
         blocks = [
@@ -239,32 +329,13 @@
         inv_col = lax.rsqrt(jnp.sum(squares, axis=1, keepdims=True) / width + EPS)
         inv = jnp.sum(jnp.where(diagonal, jnp.broadcast_to(inv_col, (seqs, seqs)), 0.0), axis=0, keepdims=True)
 
-        def all_of(phase, dst_ref, count):
-            return pltpu.make_async_remote_copy(
-                src_ref=dst_ref.at[pl.ds(0, count)], dst_ref=dst_ref.at[pl.ds(0, count)],
-                send_sem=send_sem.at[phase], recv_sem=recv_sem.at[phase],
-                device_id=device(0, 1 - core), device_id_type=MESH,
-            )
+        of_seq = lax.rem(iota((seqs, LANES), 1), seqs) == iota((seqs, LANES), 0)
+        inv_lanes = jnp.sum(jnp.where(of_seq, jnp.broadcast_to(inv_col, (seqs, LANES)), 0.0), axis=0, keepdims=True)
 
         @pl.when(core == 1)
         def _():
-            for j, ref in ((0, side), (1, bcw)):
-                lend(j, ref).wait_recv()
-            both = 2 * bc_dev
-            base = jnp.concatenate([side[0, 0], side[1, 0]], axis=0)[:, :seqs]
-            tap = jnp.concatenate([side[0, 1], side[1, 1]], axis=0)[:, :seqs]
-            weights = jnp.concatenate([bcw[0], bcw[1]], axis=0)
-            proj = dot_nt(weights[:, : width // 2], xn[:, : width // 2]) + dot_nt(weights[:, width // 2 :], xn[:, width // 2 :])
-            bc_conv = silu(base + (proj * inv).astype(BF16).astype(F32) * tap).astype(BF16).astype(F32)
-            spread = jnp.concatenate([bc_conv, jnp.zeros((both, LANES - seqs), F32)], axis=1)
-            spread = pltpu.roll(spread.reshape(both // SUBS, SUBS, LANES), 0, 2, stride=seqs, stride_axis=1)
-            bc_send[...] = jnp.sum(spread, axis=1)
-            for step, which in [(step, which) for step in steps_far for which in (0, 1)] + [(0, 0)]:
-                pltpu.make_async_remote_copy(
-                    src_ref=bc_send, dst_ref=bc_recv.at[chip], send_sem=send_sem.at[1], recv_sem=recv_sem.at[1],
-                    device_id=device(step, which), device_id_type=MESH,
-                ).start()
-            bc_recv[chip] = bc_send[...]
+            all_of(1, bc_sums, chips - 1).wait_recv()
+            relay_sums().start()
 
         dt_proj = (dot_nt(dtw[...], xn[...]) * inv).astype(BF16).astype(F32)
         loads["x_w"].wait()
@@ -291,22 +362,22 @@
 
         @pl.when(core == 0)
         def _():
-            all_of(1, bc_recv, chips).wait_recv()
-
-        @pl.when(core == 1)
-        def _():
-            all_of(1, bc_recv, chips - 1).wait_recv()
-
+            all_of(1, bc_sums, chips).wait_recv()
+
+        sums = bc_sums[0, 0:lines, :]
+        for c in range(1, chips):
+            sums = sums + bc_sums[c, 0:lines, :]
+        base, tap = [
+            jnp.concatenate([bc_sums[c, at : at + own_lines, :] for c in range(chips)], axis=0)
+            for at in (lines, lines + own_lines)
+        ]
+        bc_conv = silu(base + (sums * inv_lanes).astype(BF16).astype(F32) * tap).astype(BF16).astype(F32)
 
         def unpacked(at):
             found = []
-            for row in range(NS // SUBS):
-                line = at // SUBS + row
-                lines = 2 * bc_dev // SUBS
-                packed = bc_recv[line // lines, pl.ds(line % lines, 1), :]
-                found.append(
-                    pltpu.roll(jnp.broadcast_to(packed, (SUBS, LANES)), 0, 1, stride=seqs, stride_axis=0)
-                )
+            for eight in range(NS // SUBS):
+                line = bc_conv[at // SUBS + eight : at // SUBS + eight + 1, :]
+                found.append(pltpu.roll(jnp.broadcast_to(line, (SUBS, LANES)), 0, 1, stride=seqs, stride_axis=0))
             return jnp.concatenate(found, axis=0)[:, :seqs]
 
         c_f, b_f = unpacked(NS), unpacked(0)
@@ -375,7 +446,7 @@
         br_recv[me] = br_send[me]
 
         x_now = dot_nt(to_slot, x_proj)
-        bc_proj = (dot_nt(bcw[core], xn[...]) * inv).astype(BF16)
+        bc_proj = (dot_nt(bcw[...], xn[...]) * inv).astype(BF16)
         bc_now = dot(dot_nt(to_slot, bc_proj).astype(BF16), mirror)
         for out, old, now in ((out_cx, cxs, x_now), (out_cbc, cbcs, bc_now)):
             held = [old[k].astype(F32) for k in range(3)]
@@ -420,17 +491,26 @@
                 device_id=device(0, 1 - core), device_id_type=MESH,
             )
 
+        @pl.when((odd == 1) & (core == 0))
+        def _():
+            all_of(3, bcw_recv, n_tp).wait_send()
+
+        @pl.when((odd == 1) & (core == 1))
+        def _():
+            all_of(3, bcw_recv, n_tp - 1).wait_send()
+
         @pl.when(core == 0)
         def _():
-            hid_sent(chips).wait_send()
-            for j, ref in ((0, side), (1, bcw)):
-                lend(j, ref).wait_send()
+            hid_sent(chips - 1).wait_send()
+            first_send(0, 1, 0, 4).wait_send()
+            lend().wait_send()
 
         @pl.when(core == 1)
         def _():
             hid_sent(chips - 1).wait_send()
             relay().wait_send()
-            all_of(1, bc_recv, others).wait_send()
+            relay_sums().wait_send()
+            all_of(1, bc_sums, chips - 1).wait_send()
 
     return body
 
@@ -464,7 +544,7 @@
         scratch_shapes=[
             pltpu.VMEM((chans, width), BF16),
             pltpu.VMEM((chans, width), BF16),
-            pltpu.VMEM((2, bc_dev, width), BF16),
+            pltpu.VMEM((bc_dev, width), BF16),
             pltpu.VMEM((heads, width), BF16),
             pltpu.VMEM((3, seqs, chans), BF16),
             pltpu.VMEM((3, seqs, bc_dev), BF16),
@@ -486,15 +566,16 @@
             pltpu.VMEM((seqs, width), BF16),
             pltpu.VMEM((n_tp, seqs, feats), BF16),
             pltpu.VMEM((2, 2, bc_dev, LANES), F32),
-            pltpu.VMEM((2 * bc_dev // SUBS, LANES), F32),
-            pltpu.VMEM((n_tp, 2 * bc_dev // SUBS, LANES), F32),
+            pltpu.VMEM((tiles, bc_dev, LANES), BF16),
+            pltpu.VMEM((n_tp, 3, bc_dev, LANES), BF16),
+            pltpu.VMEM((n_tp // 2, (n_tp + 4) * bc_dev // SUBS, LANES), F32),
             pltpu.VMEM((n_tp, seqs + SUBS, LANES), BF16),
             pltpu.VMEM((n_tp, seqs + SUBS, LANES), BF16),
             pltpu.SemaphoreType.DMA((20 + 1,)),
-            pltpu.SemaphoreType.DMA((3,)),
-            pltpu.SemaphoreType.DMA((3,)),
-            pltpu.SemaphoreType.DMA((1,)),
-            pltpu.SemaphoreType.DMA((2, 2)),
+            pltpu.SemaphoreType.DMA((5,)),
+            pltpu.SemaphoreType.DMA((5,)),
+            pltpu.SemaphoreType.DMA((2,)),
+            pltpu.SemaphoreType.DMA((2,)),
         ],
         compiler_params=pltpu.CompilerParams(
             collective_id=0, has_side_effects=True, vmem_limit_bytes=60 * 1024 * 1024

time: 37.2 us -> 36.2 us (0.973)
  Pallas kernels: 36.4 us -> 35.4 us
    pallas_call x1, Pallas kernels: 34.8 us -> 33.9 us  [shards(): pl.pallas_call(make_kernel(n_tp, seqs, feats, heads, chans, bc_dev), out_...]
where the time goes in v7:
time: 36.2 us; the launch traced here: 36.1 us
  Pallas kernels  35.4 us (98%)
  between operations  0.65 us (2%)
    pallas_call x1, Pallas kernels, shards(): pl.pallas_call(make_kernel(n_tp, seqs, feats, heads, chans, bc_dev), out_...  33.9 us
    pallas_call x1, Pallas kernels, shards(): pl.pallas_call(put_out, out_shape=tuple((shape(dims, kind) for dims, kind...  1.55 us

profile of v7, /device:TPU:513, one launch (start us, length us, event | category | flops | bytes accessed | tf_op | source)
XLA Modules:
  0.0 36.1 jit_solution(14460404858427109357)
XLA Ops:
  0.6 33.9 %step.1 = (bf16[16,160]{1,0:T(8,128)(2,1)S(1)}, bf16[3,16,320]{2,1,0:T(8,128)(2,1)S(1)}, bf16[3,16,16]{2,1,0:T(8,128)(2,1)S(1)}, f32[16,320,128]{2,1,0:T(8,128)S(1)}) custom-call(bf16[16,160]{1,0:T(8,128)(2,1)} %hid.1, s32[1,16]{1,0:T(1,128)} %slot.1, s32[1,16]{1,0:T(1,128)} %bitcast.21, f32[20,128]{1,0:T(8,128)} %bitcast.19, bf16[320,2560]{1,0:T(8,128)(2,1)} %bitcast.14, ...), custom_call_target="tpu_custom_call" | custom-call | tf_op jit(solution)/shard_map/step/pallas_call | solution.py:539
  34.5 1.6 %put.1 = (bf16[16,160]{1,0:T(8,128)(2,1)}, bf16[3,16,320]{2,1,0:T(8,128)(2,1)}, bf16[3,16,16]{2,1,0:T(8,128)(2,1)}, f32[16,320,128]{2,1,0:T(8,128)}) custom-call(bf16[16,160]{1,0:T(8,128)(2,1)S(1)} %get-tuple-element.12.refs_0_, bf16[3,16,320]{2,1,0:T(8,128)(2,1)S(1)} %get-tuple-element.13.refs_1_, bf16[3,16,16]{2,1,0:T(8,128)(2,1)S(1)} %get-tuple-element.14.refs_2_, ...), custom_call_target="tpu_custom_call" | custom-call | tf_op jit(solution)/shard_map/put/pallas_call | solution.py:592

commit v8 on v7

--- a/solution.py
+++ b/solution.py
@@ -81,7 +81,7 @@
         out_layer, out_cx, out_cbc, out_state,
         zw, xw, bcw, dtw, cxs, cbcs, st, ow, gain, slot_v, slot_m, act_v, cxw, cxb, cbcw, cbcb, ngain,
         dtb_m, rate_m, skip_m,
-        stb, xn, hid_recv, side, bcw_send, bcw_recv, bc_sums, br_send, br_recv,
+        stb, xn, hid_recv, side, bcw_send, bcw_recv, bc_sums, bc_made, br_send, br_recv,
         in_sem, send_sem, recv_sem, relay_sem, side_sem,
     ):
         me = lax.axis_index("tp")
@@ -162,14 +162,6 @@
             first_send(0, 1, 0, 4).start()
             for step in steps_far:
                 first_send(step, 1, 2 * (chips - step)).start()
-
-        @pl.when(core == 1)
-        def _():
-            loads["hid"].wait()
-            pl.semaphore_wait(barrier, chips + odd * chips)
-            pl.semaphore_signal(barrier, inc=1, device_id=device(0, 0), device_id_type=MESH)
-            for step in steps_far:
-                first_send(step, 1, 2 * (chips - step) + 1).start()
 
         for name in ("slot", "slot_m", "act", "in_gain", "cbc_s", "cbc_w", "cbc_b"):
             loads[name].wait()
@@ -218,21 +210,6 @@
                 device_id={"tp": 2 * of_chip + 1, "dp": to_row}, device_id_type=MESH,
             )
 
-        @pl.when(odd == 1)
-        def _():
-            for step in steps_far:
-                for to_row in (row - 1, row):
-                    share(lax.rem(chip + step, chips), to_row).start()
-            share(chip, row - 1).start()
-
-            @pl.when(core == 0)
-            def _():
-                share(chip, row).start()
-
-            @pl.when(core == 1)
-            def _():
-                bcw_recv[me] = bcw_send[pl.ds(share_tile(chip), 3)]
-
         for name in ("cx_s", "cx_w", "cx_b", "norm_gain", "dt_bias", "log_rate", "skip_gain"):
             loads[name].wait()
         eye_ch = eye(chans)
@@ -254,6 +231,30 @@
         lax.fori_loop(0, seqs, narrow, 0)
         loads["dt_w"].wait()
 
+        @pl.when(core == 1)
+        def _():
+            loads["hid"].wait()
+            pl.semaphore_wait(barrier, chips + odd * chips)
+            pl.semaphore_signal(barrier, inc=1, device_id=device(0, 0), device_id_type=MESH)
+            for step in steps_far:
+                first_send(step, 1, 2 * (chips - step) + 1).start()
+
+        @pl.when(odd == 1)
+        def _():
+            for step in steps_far:
+                for to_row in (row - 1, row):
+                    share(lax.rem(chip + step, chips), to_row).start()
+            share(chip, row - 1).start()
+
+            @pl.when(core == 0)
+            def _():
+                share(chip, row).start()
+
+            @pl.when(core == 1)
+            def _():
+                bcw_recv[me] = bcw_send[pl.ds(share_tile(chip), 3)]
+
+
         def all_of(phase, dst_ref, count):
             return pltpu.make_async_remote_copy(
                 src_ref=dst_ref.at[pl.ds(0, count)], dst_ref=dst_ref.at[pl.ds(0, count)],
@@ -270,9 +271,9 @@
             spread = pltpu.roll(spread.reshape(count // SUBS, SUBS, LANES), 0, 2, stride=seqs, stride_axis=1)
             return jnp.sum(spread, axis=1)
 
-        def relay_sums():
+        def relay_made():
             return pltpu.make_async_remote_copy(
-                src_ref=bc_sums, dst_ref=bc_sums, send_sem=relay_sem.at[1], recv_sem=recv_sem.at[1],
+                src_ref=bc_made, dst_ref=bc_made, send_sem=relay_sem.at[1], recv_sem=recv_sem.at[1],
                 device_id=device(0, 0), device_id_type=MESH,
             )
 
@@ -332,11 +333,6 @@
         of_seq = lax.rem(iota((seqs, LANES), 1), seqs) == iota((seqs, LANES), 0)
         inv_lanes = jnp.sum(jnp.where(of_seq, jnp.broadcast_to(inv_col, (seqs, LANES)), 0.0), axis=0, keepdims=True)
 
-        @pl.when(core == 1)
-        def _():
-            all_of(1, bc_sums, chips - 1).wait_recv()
-            relay_sums().start()
-
         dt_proj = (dot_nt(dtw[...], xn[...]) * inv).astype(BF16).astype(F32)
         loads["x_w"].wait()
         loads["z_w"].wait()
@@ -360,18 +356,25 @@
         decay = per_channel(decays)
         skipped = jnp.concatenate([jnp.full((HP, seqs), skip_m[h], F32) for h in range(heads)], axis=0) * x_f
 
+        @pl.when(core == 1)
+        def _():
+            all_of(1, bc_sums, chips - 1).wait_recv()
+            sums = bc_sums[0, 0:lines, :]
+            for c in range(1, chips):
+                sums = sums + bc_sums[c, 0:lines, :]
+            base, tap = [
+                jnp.concatenate([bc_sums[c, at : at + own_lines, :] for c in range(chips)], axis=0)
+                for at in (lines, lines + own_lines)
+            ]
+            made = silu(base + (sums * inv_lanes).astype(BF16).astype(F32) * tap)
+            bc_made[...] = made.astype(BF16).astype(F32)
+            relay_made().start()
+
         @pl.when(core == 0)
         def _():
-            all_of(1, bc_sums, chips).wait_recv()
-
-        sums = bc_sums[0, 0:lines, :]
-        for c in range(1, chips):
-            sums = sums + bc_sums[c, 0:lines, :]
-        base, tap = [
-            jnp.concatenate([bc_sums[c, at : at + own_lines, :] for c in range(chips)], axis=0)
-            for at in (lines, lines + own_lines)
-        ]
-        bc_conv = silu(base + (sums * inv_lanes).astype(BF16).astype(F32) * tap).astype(BF16).astype(F32)
+            relay_made().wait_recv()
+
+        bc_conv = bc_made[...]
 
         def unpacked(at):
             found = []
@@ -509,7 +512,7 @@
         def _():
             hid_sent(chips - 1).wait_send()
             relay().wait_send()
-            relay_sums().wait_send()
+            relay_made().wait_send()
             all_of(1, bc_sums, chips - 1).wait_send()
 
     return body
@@ -569,6 +572,7 @@
             pltpu.VMEM((tiles, bc_dev, LANES), BF16),
             pltpu.VMEM((n_tp, 3, bc_dev, LANES), BF16),
             pltpu.VMEM((n_tp // 2, (n_tp + 4) * bc_dev // SUBS, LANES), F32),
+            pltpu.VMEM((n_tp * bc_dev // SUBS, LANES), F32),
             pltpu.VMEM((n_tp, seqs + SUBS, LANES), BF16),
             pltpu.VMEM((n_tp, seqs + SUBS, LANES), BF16),
             pltpu.SemaphoreType.DMA((20 + 1,)),

time: 36.2 us -> 35.7 us (0.986)
  Pallas kernels: 35.4 us -> 35 us
    pallas_call x1, Pallas kernels: 33.9 us -> 33.4 us  [shards(): pl.pallas_call(make_kernel(n_tp, seqs, feats, heads, chans, bc_dev), out_...]
where the time goes in v8:
time: 35.7 us; the launch traced here: 35.6 us
  Pallas kernels  35 us (98%)
  between operations  0.65 us (2%)
    pallas_call x1, Pallas kernels, shards(): pl.pallas_call(make_kernel(n_tp, seqs, feats, heads, chans, bc_dev), out_...  33.4 us
    pallas_call x1, Pallas kernels, shards(): pl.pallas_call(put_out, out_shape=tuple((shape(dims, kind) for dims, kind...  1.55 us

profile of v8, /device:TPU:513, one launch (start us, length us, event | category | flops | bytes accessed | tf_op | source)
XLA Modules:
  0.0 35.6 jit_solution(9405642816179335424)
XLA Ops:
  0.6 33.4 %step.1 = (bf16[16,160]{1,0:T(8,128)(2,1)S(1)}, bf16[3,16,320]{2,1,0:T(8,128)(2,1)S(1)}, bf16[3,16,16]{2,1,0:T(8,128)(2,1)S(1)}, f32[16,320,128]{2,1,0:T(8,128)S(1)}) custom-call(bf16[16,160]{1,0:T(8,128)(2,1)} %hid.1, s32[1,16]{1,0:T(1,128)} %slot.1, s32[1,16]{1,0:T(1,128)} %bitcast.21, f32[20,128]{1,0:T(8,128)} %bitcast.19, bf16[320,2560]{1,0:T(8,128)(2,1)} %bitcast.14, ...), custom_call_target="tpu_custom_call" | custom-call | tf_op jit(solution)/shard_map/step/pallas_call | solution.py:542
  34.1 1.6 %put.1 = (bf16[16,160]{1,0:T(8,128)(2,1)}, bf16[3,16,320]{2,1,0:T(8,128)(2,1)}, bf16[3,16,16]{2,1,0:T(8,128)(2,1)}, f32[16,320,128]{2,1,0:T(8,128)}) custom-call(bf16[16,160]{1,0:T(8,128)(2,1)S(1)} %get-tuple-element.12.refs_0_, bf16[3,16,320]{2,1,0:T(8,128)(2,1)S(1)} %get-tuple-element.13.refs_1_, bf16[3,16,16]{2,1,0:T(8,128)(2,1)S(1)} %get-tuple-element.14.refs_2_, ...), custom_call_target="tpu_custom_call" | custom-call | tf_op jit(solution)/shard_map/put/pallas_call | solution.py:596

commit v9 on v8

--- a/solution.py
+++ b/solution.py
@@ -81,7 +81,7 @@
         out_layer, out_cx, out_cbc, out_state,
         zw, xw, bcw, dtw, cxs, cbcs, st, ow, gain, slot_v, slot_m, act_v, cxw, cxb, cbcw, cbcb, ngain,
         dtb_m, rate_m, skip_m,
-        stb, xn, hid_recv, side, bcw_send, bcw_recv, bc_sums, bc_made, br_send, br_recv,
+        stb, xn, hid_recv, side, bcw_send, bcw_recv, bc_sums, bc_made, br_far, br_send, br_recv,
         in_sem, send_sem, recv_sem, relay_sem, side_sem,
     ):
         me = lax.axis_index("tp")
@@ -142,15 +142,16 @@
         load("out_w", out_w, ow)
 
         def first_send(step, which, dst_slot, phase=0):
+            arrival = 5 if step == half else phase
             return pltpu.make_async_remote_copy(
                 src_ref=hid_recv.at[core], dst_ref=hid_recv.at[dst_slot],
-                send_sem=send_sem.at[phase], recv_sem=recv_sem.at[phase],
+                send_sem=send_sem.at[phase], recv_sem=recv_sem.at[arrival],
                 device_id=device(step, which), device_id_type=MESH,
             )
 
-        def relay():
+        def relay(first=1, count=n_tp - 1):
             return pltpu.make_async_remote_copy(
-                src_ref=hid_recv.at[pl.ds(1, n_tp - 1)], dst_ref=hid_recv.at[pl.ds(1, n_tp - 1)],
+                src_ref=hid_recv.at[pl.ds(first, count)], dst_ref=hid_recv.at[pl.ds(first, count)],
                 send_sem=relay_sem.at[0], recv_sem=recv_sem.at[0],
                 device_id=device(0, 0), device_id_type=MESH,
             )
@@ -179,7 +180,7 @@
         row_at, col_at = iota((bc_dev, bc_dev), 0), iota((bc_dev, bc_dev), 1)
         mirror = one_hot(col_at == row_at // SUBS * SUBS + lax.rem(SUBS - lax.rem(row_at, SUBS), SUBS))
         bc_cols = dot_nt(mirror, bc_rows.astype(BF16))
-        bc_old = [dot_nt(mirror, dot(to_seq, cbcs[k]).astype(BF16)) for k in range(3)]
+        bc_old = [dot(dot_nt(mirror, cbcs[k]).astype(BF16), to_slot) for k in range(3)]
         bc_base = (bc_old[0] * bc_cols[:, 0:1] + bc_old[1] * bc_cols[:, 1:2]) + bc_old[2] * bc_cols[:, 2:3]
         pad = jnp.zeros((bc_dev, LANES - seqs), F32)
         side[core, 0] = jnp.concatenate([bc_base + bc_cols[:, 4:5], pad], axis=1)
@@ -220,7 +221,7 @@
         rows = jnp.concatenate([cxw[...].astype(F32), cxb[...].astype(F32).reshape(1, chans), g1, g2, g3], axis=0)
         cols = dot_nt(eye_ch, rows.astype(BF16))
         gain_col = (cols[:, 5:6] + cols[:, 6:7]) + cols[:, 7:8]
-        x_old = [dot_nt(eye_ch, dot(to_seq, cxs[k]).astype(BF16)) for k in range(3)]
+        x_old = [dot(dot_nt(eye_ch, cxs[k]).astype(BF16), to_slot) for k in range(3)]
         x_base = (x_old[0] * cols[:, 0:1] + x_old[1] * cols[:, 1:2]) + x_old[2] * cols[:, 2:3]
         loads["state"].wait()
 
@@ -313,8 +314,15 @@
 
         @pl.when(core == 1)
         def _():
-            all_of(0, hid_recv, n_tp - 2).wait_recv()
-            relay().start()
+            all_of(0, hid_recv, n_tp - 4).wait_recv()
+            relay(1, 2 * half - 1).start()
+            relay(2 * half + 2, n_tp - 2 * half - 2).start()
+            pltpu.make_async_remote_copy(
+                src_ref=hid_recv.at[pl.ds(2 * half, 2)], dst_ref=hid_recv.at[pl.ds(2 * half, 2)],
+                send_sem=send_sem.at[0], recv_sem=recv_sem.at[5],
+                device_id=device(half, 1), device_id_type=MESH,
+            ).wait_recv()
+            relay(2 * half, 2).start()
 
         blocks = [
             hid_recv[2 * lax.rem(t // 2 - chip + chips, chips) + t % 2].astype(F32) for t in range(n_tp)
@@ -338,24 +346,6 @@
         loads["z_w"].wait()
         x_proj = (dot_nt(xw[...], xn[...]) * inv).astype(BF16)
         z_proj = (dot_nt(zw[...], xn[...]) * inv).astype(BF16)
-        x_conv = silu(x_base + x_proj.astype(F32) * cols[:, 3:4] + cols[:, 4:5]).astype(BF16)
-        x_f = x_conv.astype(F32)
-        z_gate = silu(z_proj.astype(F32))
-        steps, decays = [], []
-        for h in range(heads):
-            raw = dt_proj[h : h + 1, :] + dtb_m[h]
-            step = jnp.maximum(raw, 0.0) + jnp.log1p(jnp.exp(-jnp.abs(raw)))
-            rate = jnp.exp(jnp.full((1, seqs), rate_m[h], F32))
-            steps.append(jnp.where(live_row, step, 0.0))
-            decays.append(jnp.where(live_row, jnp.exp(-step * rate), 1.0))
-
-        def per_channel(values):
-            return jnp.concatenate([jnp.broadcast_to(v, (HP, seqs)) for v in values], axis=0)
-
-        dtx = per_channel(steps) * x_f
-        decay = per_channel(decays)
-        skipped = jnp.concatenate([jnp.full((HP, seqs), skip_m[h], F32) for h in range(heads)], axis=0) * x_f
-
         @pl.when(core == 1)
         def _():
             all_of(1, bc_sums, chips - 1).wait_recv()
@@ -391,6 +381,23 @@
             s_big = jnp.concatenate([stb[b, at : at + chans // 2, :] for b in range(seqs)], axis=1)
             s_c.append(dot(s_big, c_big))
         s_c = jnp.concatenate(s_c, axis=0)
+        x_conv = silu(x_base + x_proj.astype(F32) * cols[:, 3:4] + cols[:, 4:5]).astype(BF16)
+        x_f = x_conv.astype(F32)
+        z_gate = silu(z_proj.astype(F32))
+        steps, decays = [], []
+        for h in range(heads):
+            raw = dt_proj[h : h + 1, :] + dtb_m[h]
+            step = jnp.maximum(raw, 0.0) + jnp.log1p(jnp.exp(-jnp.abs(raw)))
+            rate = jnp.exp(jnp.full((1, seqs), rate_m[h], F32))
+            steps.append(jnp.where(live_row, step, 0.0))
+            decays.append(jnp.where(live_row, jnp.exp(-step * rate), 1.0))
+
+        def per_channel(values):
+            return jnp.concatenate([jnp.broadcast_to(v, (HP, seqs)) for v in values], axis=0)
+
+        dtx = per_channel(steps) * x_f
+        decay = per_channel(decays)
+        skipped = jnp.concatenate([jnp.full((HP, seqs), skip_m[h], F32) for h in range(heads)], axis=0) * x_f
         bc_dot = jnp.sum(b_f * c_f, axis=0, keepdims=True)
         y = (decay * s_c + dtx * bc_dot) + skipped
         gated = y * z_gate
@@ -412,8 +419,35 @@
             tails[start] = tail
 
         def within(at):
-            at = at % LANES
+            at = lax.rem(at, LANES)
             return (lane_at >= at) & (lane_at < at + spare)
+
+        def folded(tile_0, tile_1, start, tail):
+            main = jnp.where(iota((seqs, LANES), 1) >= start, tile_0, tile_1)
+            rest = jnp.where(within(start + spare), pltpu.roll(tile_1[SUBS:], spare, 1), tail)
+            rest = jnp.where(within(start), tile_1[:SUBS], rest)
+            return jnp.concatenate([main, rest], axis=0).astype(BF16)
+
+        def window_send(src, peer):
+            pltpu.make_async_remote_copy(
+                src_ref=src, dst_ref=br_recv.at[me], send_sem=send_sem.at[2], recv_sem=recv_sem.at[2],
+                device_id={"tp": peer}, device_id_type=MESH,
+            ).start()
+
+        opposite = lax.rem(chip + half, chips)
+        far_tile = share_tile(opposite)
+        far_start = lax.rem(opposite * 2 * feats, LANES)
+        far_branch = [
+            dot(rows_seq, ow[:, pl.ds(pl.multiple_of((far_tile + k) * LANES, LANES), LANES)]) for k in range(3)
+        ]
+        for j in range(2):
+            begin = far_start + (j * feats) % LANES
+            tail = jnp.zeros((SUBS, LANES), F32)
+            for at, found in tails.items():
+                tail = jnp.where(begin == at, found, tail)
+            br_far[j] = folded(far_branch[j], far_branch[j + 1], begin, tail)
+        for j in (0, 1):
+            window_send(br_far.at[j], 2 * opposite + j)
 
         side_of = chip // half
         half_width = half * 2 * feats
@@ -431,21 +465,14 @@
                 first, start = (i * feats) // LANES, (i * feats) % LANES
                 tile_0 = branch[:, first * LANES : (first + 1) * LANES]
                 tile_1 = branch[:, (first + 1) * LANES : (first + 2) * LANES]
-                main = jnp.where(iota((seqs, LANES), 1) >= start, tile_0, tile_1)
-                rest = jnp.where(within(start + spare), pltpu.roll(tile_1[SUBS:], spare, 1), tails[start])
-                rest = jnp.where(within(start), tile_1[:SUBS], rest)
-                br_send[which * 2 * half + i] = jnp.concatenate([main, rest], axis=0).astype(BF16)
-            for i in range(half):
+                br_send[which * 2 * half + i] = folded(tile_0, tile_1, start, tails[start])
+            for i in range(1 - part, half):
                 far = which * half + lax.rem(chip + i, half)
                 for flip in (1, 0):
                     if part == 1 and i == 0 and not flip:
                         continue
                     peer = far * 2 + (1 - core if flip else core)
-                    pltpu.make_async_remote_copy(
-                        src_ref=br_send.at[peer], dst_ref=br_recv.at[me],
-                        send_sem=send_sem.at[2], recv_sem=recv_sem.at[2],
-                        device_id={"tp": peer}, device_id_type=MESH,
-                    ).start()
+                    window_send(br_send.at[peer], peer)
         br_recv[me] = br_send[me]
 
         x_now = dot_nt(to_slot, x_proj)
@@ -573,11 +600,12 @@
             pltpu.VMEM((n_tp, 3, bc_dev, LANES), BF16),
             pltpu.VMEM((n_tp // 2, (n_tp + 4) * bc_dev // SUBS, LANES), F32),
             pltpu.VMEM((n_tp * bc_dev // SUBS, LANES), F32),
+            pltpu.VMEM((2, seqs + SUBS, LANES), BF16),
             pltpu.VMEM((n_tp, seqs + SUBS, LANES), BF16),
             pltpu.VMEM((n_tp, seqs + SUBS, LANES), BF16),
             pltpu.SemaphoreType.DMA((20 + 1,)),
             pltpu.SemaphoreType.DMA((5,)),
-            pltpu.SemaphoreType.DMA((5,)),
+            pltpu.SemaphoreType.DMA((6,)),
             pltpu.SemaphoreType.DMA((2,)),
             pltpu.SemaphoreType.DMA((2,)),
         ],

time: 35.7 us -> 35.9 us (level)
  no operation moved by 1% of the time
where the time goes in v9:
time: 35.9 us; the launch traced here: 35.8 us
  Pallas kernels  35.1 us (98%)
  between operations  0.65 us (2%)
    pallas_call x1, Pallas kernels, shards(): pl.pallas_call(make_kernel(n_tp, seqs, feats, heads, chans, bc_dev), out_...  33.6 us
    pallas_call x1, Pallas kernels, shards(): pl.pallas_call(put_out, out_shape=tuple((shape(dims, kind) for dims, kind...  1.55 us

profile of v9, /device:TPU:513, one launch (start us, length us, event | category | flops | bytes accessed | tf_op | source)
XLA Modules:
  0.0 35.8 jit_solution(10441962652436764442)
XLA Ops:
  0.6 33.6 %step.1 = (bf16[16,160]{1,0:T(8,128)(2,1)S(1)}, bf16[3,16,320]{2,1,0:T(8,128)(2,1)S(1)}, bf16[3,16,16]{2,1,0:T(8,128)(2,1)S(1)}, f32[16,320,128]{2,1,0:T(8,128)S(1)}) custom-call(bf16[16,160]{1,0:T(8,128)(2,1)} %hid.1, s32[1,16]{1,0:T(1,128)} %slot.1, s32[1,16]{1,0:T(1,128)} %bitcast.21, f32[20,128]{1,0:T(8,128)} %bitcast.19, bf16[320,2560]{1,0:T(8,128)(2,1)} %bitcast.14, ...), custom_call_target="tpu_custom_call" | custom-call | tf_op jit(solution)/shard_map/step/pallas_call | solution.py:569
  34.2 1.6 %put.1 = (bf16[16,160]{1,0:T(8,128)(2,1)}, bf16[3,16,320]{2,1,0:T(8,128)(2,1)}, bf16[3,16,16]{2,1,0:T(8,128)(2,1)}, f32[16,320,128]{2,1,0:T(8,128)}) custom-call(bf16[16,160]{1,0:T(8,128)(2,1)S(1)} %get-tuple-element.12.refs_0_, bf16[3,16,320]{2,1,0:T(8,128)(2,1)S(1)} %get-tuple-element.13.refs_1_, bf16[3,16,16]{2,1,0:T(8,128)(2,1)S(1)} %get-tuple-element.14.refs_2_, ...), custom_call_target="tpu_custom_call" | custom-call | tf_op jit(solution)/shard_map/put/pallas_call | solution.py:624

commit v10 on v9

--- a/solution.py
+++ b/solution.py
@@ -81,7 +81,7 @@
         out_layer, out_cx, out_cbc, out_state,
         zw, xw, bcw, dtw, cxs, cbcs, st, ow, gain, slot_v, slot_m, act_v, cxw, cxb, cbcw, cbcb, ngain,
         dtb_m, rate_m, skip_m,
-        stb, xn, hid_recv, side, bcw_send, bcw_recv, bc_sums, bc_made, br_far, br_send, br_recv,
+        stb, xn, hid_recv, side, bcw_send, bcw_recv, bc_sums, bc_made, br_send, br_recv,
         in_sem, send_sem, recv_sem, relay_sem, side_sem,
     ):
         me = lax.axis_index("tp")
@@ -434,44 +434,23 @@
                 device_id={"tp": peer}, device_id_type=MESH,
             ).start()
 
-        opposite = lax.rem(chip + half, chips)
-        far_tile = share_tile(opposite)
-        far_start = lax.rem(opposite * 2 * feats, LANES)
-        far_branch = [
-            dot(rows_seq, ow[:, pl.ds(pl.multiple_of((far_tile + k) * LANES, LANES), LANES)]) for k in range(3)
-        ]
-        for j in range(2):
-            begin = far_start + (j * feats) % LANES
-            tail = jnp.zeros((SUBS, LANES), F32)
-            for at, found in tails.items():
-                tail = jnp.where(begin == at, found, tail)
-            br_far[j] = folded(far_branch[j], far_branch[j + 1], begin, tail)
-        for j in (0, 1):
-            window_send(br_far.at[j], 2 * opposite + j)
-
-        side_of = chip // half
-        half_width = half * 2 * feats
-        for part in range(2):
-            which = 1 - side_of if part == 0 else side_of
-            step = 2 * LANES
-            branch = jnp.concatenate(
-                [
-                    dot(rows_seq, ow[:, pl.ds(pl.multiple_of(which * half_width + at, LANES), step)])
-                    for at in range(0, half_width, step)
-                ],
-                axis=1,
-            )
-            for i in range(2 * half):
-                first, start = (i * feats) // LANES, (i * feats) % LANES
-                tile_0 = branch[:, first * LANES : (first + 1) * LANES]
-                tile_1 = branch[:, (first + 1) * LANES : (first + 2) * LANES]
-                br_send[which * 2 * half + i] = folded(tile_0, tile_1, start, tails[start])
-            for i in range(1 - part, half):
-                far = which * half + lax.rem(chip + i, half)
-                for flip in (1, 0):
-                    if part == 1 and i == 0 and not flip:
-                        continue
-                    peer = far * 2 + (1 - core if flip else core)
+        def windows(step):
+            to = lax.rem(chip + step, chips)
+            first, start = share_tile(to), lax.rem(to * 2 * feats, LANES)
+            branch = [dot(rows_seq, ow[:, pl.ds(pl.multiple_of((first + k) * LANES, LANES), LANES)]) for k in range(3)]
+            for j in range(2):
+                begin = start + (j * feats) % LANES
+                tail = jnp.zeros((SUBS, LANES), F32)
+                for at, found in tails.items():
+                    tail = jnp.where(begin == at, found, tail)
+                br_send[2 * to + j] = folded(branch[j], branch[j + 1], begin, tail)
+
+        for group in ([half], [half - 1, half + 1], [k for k in steps_far if abs(k - half) > 1] + [0]):
+            for step in group:
+                windows(step)
+            for step in group:
+                for which in (0, 1) if step else (1 - core,):
+                    peer = lax.rem(chip + step, chips) * 2 + which
                     window_send(br_send.at[peer], peer)
         br_recv[me] = br_send[me]
 
@@ -600,7 +579,6 @@
             pltpu.VMEM((n_tp, 3, bc_dev, LANES), BF16),
             pltpu.VMEM((n_tp // 2, (n_tp + 4) * bc_dev // SUBS, LANES), F32),
             pltpu.VMEM((n_tp * bc_dev // SUBS, LANES), F32),
-            pltpu.VMEM((2, seqs + SUBS, LANES), BF16),
             pltpu.VMEM((n_tp, seqs + SUBS, LANES), BF16),
             pltpu.VMEM((n_tp, seqs + SUBS, LANES), BF16),
             pltpu.SemaphoreType.DMA((20 + 1,)),

time: 35.9 us -> 35.8 us (level)
  no operation moved by 1% of the time
where the time goes in v10:
time: 35.8 us; the launch traced here: 35.7 us
  Pallas kernels  35.1 us (98%)
  between operations  0.65 us (2%)
    pallas_call x1, Pallas kernels, shards(): pl.pallas_call(make_kernel(n_tp, seqs, feats, heads, chans, bc_dev), out_...  33.5 us
    pallas_call x1, Pallas kernels, shards(): pl.pallas_call(put_out, out_shape=tuple((shape(dims, kind) for dims, kind...  1.55 us

profile of v10, /device:TPU:513, one launch (start us, length us, event | category | flops | bytes accessed | tf_op | source)
XLA Modules:
  0.0 35.7 jit_solution(11255339238272586678)
XLA Ops:
  0.6 33.5 %step.1 = (bf16[16,160]{1,0:T(8,128)(2,1)S(1)}, bf16[3,16,320]{2,1,0:T(8,128)(2,1)S(1)}, bf16[3,16,16]{2,1,0:T(8,128)(2,1)S(1)}, f32[16,320,128]{2,1,0:T(8,128)S(1)}) custom-call(bf16[16,160]{1,0:T(8,128)(2,1)} %hid.1, s32[1,16]{1,0:T(1,128)} %slot.1, s32[1,16]{1,0:T(1,128)} %bitcast.21, f32[20,128]{1,0:T(8,128)} %bitcast.19, bf16[320,2560]{1,0:T(8,128)(2,1)} %bitcast.14, ...), custom_call_target="tpu_custom_call" | custom-call | tf_op jit(solution)/shard_map/step/pallas_call | solution.py:548
  34.2 1.6 %put.1 = (bf16[16,160]{1,0:T(8,128)(2,1)}, bf16[3,16,320]{2,1,0:T(8,128)(2,1)}, bf16[3,16,16]{2,1,0:T(8,128)(2,1)}, f32[16,320,128]{2,1,0:T(8,128)}) custom-call(bf16[16,160]{1,0:T(8,128)(2,1)S(1)} %get-tuple-element.12.refs_0_, bf16[3,16,320]{2,1,0:T(8,128)(2,1)S(1)} %get-tuple-element.13.refs_1_, bf16[3,16,16]{2,1,0:T(8,128)(2,1)S(1)} %get-tuple-element.14.refs_2_, ...), custom_call_target="tpu_custom_call" | custom-call | tf_op jit(solution)/shard_map/put/pallas_call | solution.py:602

commit v11 on v10

--- a/solution.py
+++ b/solution.py
@@ -449,7 +449,7 @@
             for step in group:
                 windows(step)
             for step in group:
-                for which in (0, 1) if step else (1 - core,):
+                for which in (1, 0) if step else (1 - core,):
                     peer = lax.rem(chip + step, chips) * 2 + which
                     window_send(br_send.at[peer], peer)
         br_recv[me] = br_send[me]
@@ -477,16 +477,16 @@
         for t in range(1, n_tp):
             total = total + br_recv[t].astype(F32)
         shift = lax.rem(me * feats, LANES)
+        sq_at = lane_at - lax.rem(shift + 2 * spare, LANES)
+        sq_rows = [
+            jnp.sum(jnp.where((sq_at == j) | (sq_at == j + 2) | (sq_at == j + 4), total[seqs:], 0.0), axis=1, keepdims=True)
+            for j in range(2)
+        ]
+        inv_out = lax.rsqrt(jnp.concatenate(sq_rows, axis=0) / INNER + EPS)
         total = pltpu.roll(total, lax.rem(LANES - shift, LANES), 1)
         rest = total[seqs:]
         rest = jnp.concatenate([rest, pltpu.roll(rest, LANES - spare, 1)], axis=0)
         branch_sum = jnp.concatenate([total[:seqs], rest[:, :spare]], axis=1)
-        sq_at = 2 * spare
-        sq_rows = [
-            (total[seqs:, at : at + 1] + total[seqs:, at + 2 : at + 3]) + total[seqs:, at + 4 : at + 5]
-            for at in (sq_at, sq_at + 1)
-        ]
-        inv_out = lax.rsqrt(jnp.concatenate(sq_rows, axis=0) / INNER + EPS)
         kept = hid_recv[core].astype(F32)
         fresh = (kept + inv_out * branch_sum).astype(BF16).astype(F32)
         out_layer[...] = jnp.where(act_col, fresh, kept).astype(BF16)

time: 35.8 us -> 35.4 us (0.989)
  Pallas kernels: 35.1 us -> 34.6 us
    pallas_call x1, Pallas kernels: 33.5 us -> 33.1 us  [shards(): pl.pallas_call(make_kernel(n_tp, seqs, feats, heads, chans, bc_dev), out_...]
where the time goes in v11:
time: 35.4 us; the launch traced here: 35.3 us
  Pallas kernels  34.6 us (98%)
  between operations  0.65 us (2%)
    pallas_call x1, Pallas kernels, shards(): pl.pallas_call(make_kernel(n_tp, seqs, feats, heads, chans, bc_dev), out_...  33.1 us
    pallas_call x1, Pallas kernels, shards(): pl.pallas_call(put_out, out_shape=tuple((shape(dims, kind) for dims, kind...  1.55 us

profile of v11, /device:TPU:513, one launch (start us, length us, event | category | flops | bytes accessed | tf_op | source)
XLA Modules:
  0.0 35.3 jit_solution(12220653300871686698)
XLA Ops:
  0.6 33.1 %step.1 = (bf16[16,160]{1,0:T(8,128)(2,1)S(1)}, bf16[3,16,320]{2,1,0:T(8,128)(2,1)S(1)}, bf16[3,16,16]{2,1,0:T(8,128)(2,1)S(1)}, f32[16,320,128]{2,1,0:T(8,128)S(1)}) custom-call(bf16[16,160]{1,0:T(8,128)(2,1)} %hid.1, s32[1,16]{1,0:T(1,128)} %slot.1, s32[1,16]{1,0:T(1,128)} %bitcast.21, f32[20,128]{1,0:T(8,128)} %bitcast.19, bf16[320,2560]{1,0:T(8,128)(2,1)} %bitcast.14, ...), custom_call_target="tpu_custom_call" | custom-call | tf_op jit(solution)/shard_map/step/pallas_call | solution.py:548
  33.7 1.6 %put.1 = (bf16[16,160]{1,0:T(8,128)(2,1)}, bf16[3,16,320]{2,1,0:T(8,128)(2,1)}, bf16[3,16,16]{2,1,0:T(8,128)(2,1)}, f32[16,320,128]{2,1,0:T(8,128)}) custom-call(bf16[16,160]{1,0:T(8,128)(2,1)S(1)} %get-tuple-element.12.refs_0_, bf16[3,16,320]{2,1,0:T(8,128)(2,1)S(1)} %get-tuple-element.13.refs_1_, bf16[3,16,16]{2,1,0:T(8,128)(2,1)S(1)} %get-tuple-element.14.refs_2_, ...), custom_call_target="tpu_custom_call" | custom-call | tf_op jit(solution)/shard_map/put/pallas_call | solution.py:602
